TPU v7x, 32 devices: a whole 2x2x4 slice. The times are simulated.
32 devices in a mesh: member: 2 (over x), dp: 8 (over z, y), mp: 2 (over core).
Axes of the slice: x: 2, y: 2, z: 4, core: 2. Of those that a mesh axis runs over, the one named last changes fastest.
Arguments:
- activations: bfloat16 [2048, 2048], P(('member', 'dp')), parts along dimension 0, may hold values from -6 to 6
- out_grads: bfloat16 [2048, 10240], P(('member', 'dp'), 'mp'), parts along dimension 0, may hold values from -0.19921875 to 0.19921875
- slot_table: int32 [4, 16], P(('member', 'mp')), parts along dimension 0, may hold values from 0 to 15, each once within a row
- exponent_index: int32 [4, 16], P(('member', 'mp')), parts along dimension 0, may hold values from 0 to 1
- damping_index: int32 [4, 16], P(('member', 'mp')), parts along dimension 0, may hold values from 0 to 3
Outputs:
- update: bfloat16 [4096, 10240], P('member', 'mp'), parts along dimension 0
- preconditioners: bfloat16 [4, 16, 2, 1024, 1024], P(('member', 'mp'), 'dp'), parts along dimension 0
There are 2 independent parts, one for each index of `member`. A program takes and returns all parts, laid end to end along the dimension named above; each array names one. Nothing has to cross between parts.
Inputs may be any that keep to these rules, and one draw needn't show every extreme that they name: `slot_table`: each row is a permutation of 0 to 15; slot s belongs to dp index s.
All inputs are finite; a program needn't handle non-finite values.
Results may differ from a plain program's by a relative error of at most 0.006.
The roundings to bfloat16 on the way count: a program that leaves them out, or rounds other values in their place, can miss the bound.
Values may be sent and summed in bfloat16 or wider, within the bound.
No kernel may reach another device: no remote copies, remote signals or barrier semaphores. Data moves between devices by JAX's collectives and lax.ppermute only.
A program may use at most 192 MiB of HBM per device.

v0:
```python
import functools

import jax
import jax.numpy as jnp
from jax import lax
from jax.experimental import pallas as pl
from jax.experimental.pallas import tpu as pltpu
from jax.sharding import PartitionSpec as P


BLK = 1024
TILE = 256
ROOT_ORDERS = (2.0, 4.0)
DAMPINGS = (0.03, 0.1, 0.3, 1.0)
HBM = pltpu.MemorySpace.HBM
VMEM_LIMIT = 60 * 2**20


def table_value(picked, values_table):
    values = jnp.asarray(values_table, jnp.float32)
    matches = jnp.arange(len(values_table), dtype=jnp.int32) == picked[:, None]
    return jnp.sum(jnp.where(matches, values, 0.0), axis=1)


def wide_dot(first, second, first_dim, second_dim):
    return lax.dot_general(
        first, second, (((first_dim,), (second_dim,)), ((), ())), preferred_element_type=jnp.float32
    )


def gather_block(ints, places, sources, acts_t, grads, sems):
    owners, turns, tok, grad_refs, act_refs = sources
    turn, column = ints[0], ints[1]
    columns = pl.ds(pl.multiple_of(column * BLK, BLK), BLK)
    half_tok = tok // 2
    half_row = BLK // 2
    waits = []

    def start(copy_of, count):
        sem = sems.at[len(waits)]
        for index in range(count):
            if count == 1:
                copy_of(index, sem).start()
            else:
                pl.when(turn == index)(lambda index=index: copy_of(index, sem).start())
        waits.append(copy_of(0, sem))

    for step in range(owners):
        for way in range(2):
            if step == 0 and way == 1:
                continue
            source = places[way * owners + step]
            rows = tok if step == 0 else half_tok
            at_tok = pl.multiple_of(source * tok + (half_tok * way), half_tok)
            at_lane = pl.multiple_of(source * tok, tok)
            grad_ref = grad_refs[step * 2 + way]
            start(
                lambda _, sem, grad_ref=grad_ref, at_tok=at_tok, rows=rows: pltpu.make_async_copy(
                    grad_ref.at[:, columns], grads.at[pl.ds(at_tok, rows), :], sem
                ),
                1,
            )
            act_rows = slice(0, BLK) if step == 0 else slice(half_row * way, half_row * (way + 1))
            start(
                lambda index, sem, at_lane=at_lane, act_rows=act_rows, at=step * 2 + way: (
                    pltpu.make_async_copy(
                        act_refs[index][at], acts_t.at[act_rows, pl.ds(at_lane, tok)], sem
                    )
                ),
                turns,
            )
    for copy in waits:
        copy.wait()


def symmetric_product(matrix, second_dim, finish, outs):
    for low in range(0, BLK, TILE):
        high = low + TILE
        second = matrix[low:, :] if second_dim else matrix[:, low:]
        tile = wide_dot(matrix[low:high, :], second, 1, second_dim)
        for out, value in zip(outs, finish(tile)):
            out[low:high, low:] = value
            if high < BLK:
                out[high:, low:high] = value[:, TILE:].T


def diagonal(shape):
    return lax.broadcasted_iota(jnp.int32, shape, 0) == lax.broadcasted_iota(jnp.int32, shape, 1)


def inverse_root(side, gradient, root, square_sum, params, current, factor, raised, later):
    root_order, quartic, damping = params
    shift = damping * (square_sum / BLK + 1.0)
    scale = BLK / (2.0 * (square_sum + BLK * shift))
    inverse = 1.0 / root_order

    def first_pair(statistic):
        eye = diagonal(statistic.shape)
        scaled = jnp.where(eye, statistic + shift, statistic) * scale
        first = (jnp.where(eye, root_order + 1.0, 0.0) - scaled) * inverse
        return scaled.astype(jnp.bfloat16), first.astype(jnp.bfloat16)

    def rounded(product):
        return (product.astype(jnp.bfloat16),)

    symmetric_product(gradient.at[side], 1, first_pair, (current, factor))
    symmetric_product(factor, 0, rounded, (raised.at[0],))

    @pl.when(quartic != 0)
    def _():
        symmetric_product(raised.at[0], 0, rounded, (raised.at[1],))

    moved = wide_dot(raised[quartic], current[...], 1, 0)
    eye = diagonal(moved.shape)
    later[...] = ((jnp.where(eye, root_order + 1.0, 0.0) - moved) * inverse).astype(jnp.bfloat16)
    root[...] = wide_dot(factor[...], later[...], 1, 0).astype(jnp.bfloat16)


def block_kernel(kind, owners, turns, extra, job, position, *refs):
    refs = list(refs)
    int_table, float_table, places = refs[:3]
    ints = [int_table[4 * job + field] for field in range(4)]
    floats = [float_table[2 * job + field] for field in range(2)]
    chunks = 2 * owners - 1
    at = 3
    own = refs[at : at + chunks]
    grad_refs = [own[0], None] + own[1:]
    at += chunks
    act_refs = []
    for _ in range(turns):
        own = refs[at : at + chunks]
        act_refs.append([own[0], None] + own[1:])
        at += chunks
    tok = grad_refs[0].shape[0]
    left_in = None
    if kind == "finish":
        left_in = refs[at]
        at += 1
    at += extra
    outs = refs[at : at + (1 if kind in ("left", "roots") else 3)]
    at += len(outs)
    acts_t, grads, gradient, current, factor, raised, later, pair, sems, out_sems = refs[at:]
    gather_block(
        ints, places, (owners, turns, tok, grad_refs, act_refs), acts_t, grads, sems
    )
    block_grad = wide_dot(acts_t[...], grads[...], 1, 0)
    block_grad = jnp.where(ints[3] != 0, block_grad, 0.0).astype(jnp.bfloat16)
    gradient[0] = block_grad
    if kind != "left":
        gradient[1] = block_grad.T
    squares = block_grad.astype(jnp.float32)
    square_sum = jnp.sum(squares * squares)
    params = (floats[0], ints[2], floats[1])
    work = (current, factor, raised, later)
    if kind == "left":
        inverse_root(0, gradient, outs[0], square_sum, params, *work)
        return
    if kind == "finish":
        inverse_root(1, gradient, pair.at[1], square_sum, params, *work)
        left_root = left_in[...]
    else:

        def one_side(side, carry):
            inverse_root(side, gradient, pair.at[side], square_sum, params, *work)
            if kind == "roots":
                pltpu.make_async_copy(
                    pair.at[side], outs[0].at[position, side], out_sems.at[side]
                ).start()
            return carry

        lax.fori_loop(0, 2, one_side, 0)
        left_root = pair[0]
    if kind == "roots":
        for side in range(2):
            pltpu.make_async_copy(
                pair.at[side], outs[0].at[position, side], out_sems.at[side]
            ).wait()
        return
    later[...] = wide_dot(left_root, gradient[0], 1, 0).astype(jnp.bfloat16)
    update = wide_dot(later[...], pair[1], 1, 0).astype(jnp.bfloat16)
    outs[0][...] = update[: BLK // 2]
    outs[1][...] = update[BLK // 2 :]
    wide = update.astype(jnp.float32)
    outs[2][0, 0] = jnp.sum(wide * wide)


def run_block(kind, job, meta, chunks, left_root=None, roots=None, position=0, count=1, after=()):
    ints, floats, places = meta
    grad_chunks, act_chunks = chunks
    owners = (len(grad_chunks) + 1) // 2
    turns = len(act_chunks)
    tokens = owners * grad_chunks[0].shape[0]
    smem = pl.BlockSpec(memory_space=pltpu.SMEM)
    vmem = pl.BlockSpec(memory_space=pltpu.VMEM)
    hbm = pl.BlockSpec(memory_space=HBM)
    operands = [ints, floats, places, *grad_chunks]
    for turn in act_chunks:
        operands += turn
    specs = [smem] * 3 + [hbm] * (len(operands) - 3)
    if left_root is not None:
        operands.append(left_root)
        specs.append(vmem)
    aliases = {}
    if roots is not None:
        aliases = {len(operands): 0}
        after = (roots, *after)
    operands += after
    specs += [hbm] * len(after)
    half = jnp.bfloat16
    piece = jax.ShapeDtypeStruct((BLK // 2, BLK), half)
    if kind == "left":
        out_shape, out_specs = jax.ShapeDtypeStruct((BLK, BLK), half), vmem
    elif kind == "roots":
        out_shape, out_specs = jax.ShapeDtypeStruct((count, 2, BLK, BLK), half), hbm
    else:
        out_shape = (piece, piece, jax.ShapeDtypeStruct((1, 1), jnp.float32))
        out_specs = (vmem, vmem, smem)
    matmuls = {"left": 6, "roots": 11, "finish": 8, "both": 13}[kind]
    return pl.pallas_call(
        functools.partial(block_kernel, kind, owners, turns, len(after), job, position),
        out_shape=out_shape,
        in_specs=specs,
        out_specs=out_specs,
        input_output_aliases=aliases,
        scratch_shapes=[
            pltpu.VMEM((BLK, tokens), half),
            pltpu.VMEM((tokens, BLK), half),
            pltpu.VMEM((2, BLK, BLK), half),
            pltpu.VMEM((BLK, BLK), half),
            pltpu.VMEM((BLK, BLK), half),
            pltpu.VMEM((2, BLK, BLK), half),
            pltpu.VMEM((BLK, BLK), half),
            pltpu.VMEM((2, BLK, BLK), half),
            pltpu.SemaphoreType.DMA((2 * (2 * owners - 1),)),
            pltpu.SemaphoreType.DMA((2,)),
        ],
        compiler_params=pltpu.CompilerParams(vmem_limit_bytes=VMEM_LIMIT),
        cost_estimate=pl.CostEstimate(
            flops=matmuls * 2 * BLK**3, bytes_accessed=6 * 2 * BLK**2, transcendentals=0
        ),
    )(*operands)


def place_kernel(first, count, extra, *refs):
    spots, rescale = refs[:2]
    pieces = refs[2 : 2 + count]
    canvas, held, in_sems, out_sems = refs[2 + count + extra :]
    rows = held.shape[1]
    loads = []
    stores = []
    for index in range(count):
        row = pl.multiple_of(spots[2 * (first + index)], rows)
        column = pl.multiple_of(spots[2 * (first + index) + 1], BLK)
        loads.append(pltpu.make_async_copy(pieces[index], held.at[index], in_sems.at[index]))
        stores.append(
            pltpu.make_async_copy(
                held.at[index],
                canvas.at[pl.ds(row, rows), pl.ds(column, BLK)],
                out_sems.at[index],
            )
        )
    for load in loads:
        load.start()
    for index in range(count):
        loads[index].wait()
        wide = held[index].astype(jnp.float32) * rescale[0, 0]
        held[index] = wide.astype(jnp.bfloat16)
        stores[index].start()
    for store in stores:
        store.wait()


def place_pieces(canvas, shape, spots, first, rescale, pieces):
    count = len(pieces)
    smem = pl.BlockSpec(memory_space=pltpu.SMEM)
    hbm = pl.BlockSpec(memory_space=HBM)
    old = [] if canvas is None else [canvas]
    return pl.pallas_call(
        functools.partial(place_kernel, first, count, len(old)),
        out_shape=jax.ShapeDtypeStruct(shape, jnp.bfloat16),
        in_specs=[smem, smem] + [hbm] * (count + len(old)),
        out_specs=hbm,
        input_output_aliases={2 + count: 0} if old else {},
        scratch_shapes=[
            pltpu.VMEM((count, *pieces[0].shape), jnp.bfloat16),
            pltpu.SemaphoreType.DMA((count,)),
            pltpu.SemaphoreType.DMA((count,)),
        ],
        compiler_params=pltpu.CompilerParams(vmem_limit_bytes=VMEM_LIMIT),
        cost_estimate=pl.CostEstimate(
            flops=count * BLK * BLK * 100, bytes_accessed=2 * count * BLK * BLK, transcendentals=0
        ),
        name="place",
    )(spots, rescale, *pieces, *old)


def ring_pairs(count):
    order = list(range(0, count, 2)) + list(range(1, count, 2))[::-1]
    ahead = [(order[i], order[(i + 1) % count]) for i in range(count)]
    back = [(b, a) for a, b in ahead]
    return order, ahead, back


def shampoo_step(activations, out_grads, slot_table, exponent_index, damping_index):
    tok_count = activations.shape[0]
    row_blocks = activations.shape[1] // BLK
    half_width = out_grads.shape[1]
    col_blocks = half_width // BLK
    half_blocks = row_blocks * col_blocks
    owners = lax.axis_size("dp")
    halves = lax.axis_size("mp")
    me = lax.axis_index("dp")
    core = lax.axis_index("mp")
    slot_count = slot_table.shape[1]
    per_owner = slot_count // owners
    order, ahead, back = ring_pairs(owners)
    order_of = jnp.asarray(order, jnp.int32)
    place = jnp.asarray([order.index(i) for i in range(owners)], jnp.int32)[me]
    steps = jnp.arange(owners, dtype=jnp.int32)
    from_behind = order_of[(place - steps) % owners]
    from_ahead = order_of[(place + steps) % owners]
    places = jnp.concatenate([from_behind, from_ahead])

    table = slot_table[0, :half_blocks]
    exponents = exponent_index[0]
    dampings = damping_index[0]

    shared = min(owners, half_blocks)
    mine = jnp.minimum(me, shared - 1)
    block_range = jnp.arange(half_blocks, dtype=jnp.int32)
    slot_range = jnp.arange(slot_count, dtype=jnp.int32)
    spread = jnp.concatenate([mine[None], block_range[shared:]])
    spread_slots = jnp.sum(
        jnp.where(spread[:, None] == block_range[None, :], table[None, :], 0), axis=1
    )
    own_slots = me * per_owner + jnp.arange(per_owner, dtype=jnp.int32)
    matches = own_slots[:, None] == table[None, :]
    own_blocks = jnp.sum(jnp.where(matches, block_range[None, :], 0), axis=1)
    blocks = jnp.concatenate([spread, own_blocks])
    slots = jnp.concatenate([spread_slots, own_slots])
    filled = jnp.concatenate([jnp.ones_like(spread), jnp.any(matches, axis=1).astype(jnp.int32)])
    at_slot = slots[:, None] == slot_range[None, :]
    exp_picks = jnp.sum(jnp.where(at_slot, exponents[None, :], 0), axis=1)
    damp_picks = jnp.sum(jnp.where(at_slot, dampings[None, :], 0), axis=1)
    turn = (core - blocks // col_blocks) % halves
    ints = jnp.stack([turn, blocks % col_blocks, exp_picks, filled], axis=1).reshape(-1)
    floats = jnp.stack(
        [table_value(exp_picks, ROOT_ORDERS), table_value(damp_picks, DAMPINGS)], axis=1
    ).reshape(-1)
    late_count = 2
    rows = BLK // 2
    put_blocks = jnp.concatenate(
        [jnp.repeat(block_range[shared:], 2), jnp.stack([from_behind, from_ahead], 1).reshape(-1)]
    )
    put_blocks = jnp.minimum(put_blocks, half_blocks - 1)
    put_lower = jnp.tile(jnp.asarray([0, rows], jnp.int32), put_blocks.shape[0] // 2)
    spots = jnp.stack(
        [(put_blocks // col_blocks) * BLK + put_lower, (put_blocks % col_blocks) * BLK], axis=1
    ).reshape(-1)
    meta = (ints.astype(jnp.int32), floats, places, spots)

    part = activations.shape[1] // halves
    assert part == BLK
    act_part = lax.dynamic_slice(activations, (0, core * part), (tok_count, part)).T
    mp_shifts = [[(i, (i + s) % halves) for i in range(halves)] for s in range(1, halves)]
    half_tok = tok_count // 2
    half_row = part // 2

    grad_chunks = [out_grads]
    act_chunks = [[act_part]]
    for shift in mp_shifts:
        act_chunks.append([lax.ppermute(act_part, "mp", shift)])
    down = (out_grads[:half_tok], act_part[:half_row])
    up = (out_grads[half_tok:], act_part[half_row:])
    for step in range(1, owners):
        down = tuple(lax.ppermute(piece, "dp", ahead) for piece in down)
        up = tuple(lax.ppermute(piece, "dp", back) for piece in up)
        if step == 2:
            down, up, meta = lax.optimization_barrier((down, up, meta))
        else:
            down, up = lax.optimization_barrier((down, up))
        grad_chunks += [down[0], up[0]]
        act_chunks[0] += [down[1], up[1]]
        for turn, shift in enumerate(mp_shifts):
            act_chunks[turn + 1] += [lax.ppermute(piece[1], "mp", shift) for piece in (down, up)]
    chunks = (grad_chunks, act_chunks)

    spots = meta[3]
    meta = meta[:3]
    upper, lower, piece_sq = run_block("both", 0, meta, chunks)
    piece_sq = jnp.where(me < shared, piece_sq, 0.0)
    downs, ups = [upper], [lower]

    jobs = []
    rest = {}
    roots = [None]
    for job, block in enumerate(range(shared, half_blocks), 1):
        jobs.append(("left", lambda after, job=job, block=block: rest.__setitem__(
            block, run_block("left", job, meta, chunks, after=after)) or rest[block]))
        jobs.append(("finish", lambda after, job=job, block=block: rest.__setitem__(
            block, run_block("finish", job, meta, chunks, left_root=rest[block], after=after))
            or rest[block][0]))
    first = 1 + half_blocks - shared
    for position in range(per_owner):
        jobs.append(("roots", lambda after, position=position: roots.__setitem__(
            0, run_block("roots", first + position, meta, chunks, roots=roots[0],
                         position=position, count=per_owner, after=after)) or roots[0]))

    def exchange(value, axis, bit):
        pairs = [(i, i ^ bit) for i in range(lax.axis_size(axis))]
        return value + lax.ppermute(value, axis, pairs)

    bits = [1 << i for i in range((owners - 1).bit_length())]
    core_bits = [1 << i for i in range((halves - 1).bit_length())]
    half_sq = piece_sq
    for step in range(1, owners):
        after = (downs[-1], ups[-1]) if step > 1 else ()
        down = lax.ppermute(downs[-1], "dp", ahead)
        up = lax.ppermute(ups[-1], "dp", back)
        kind = jobs[0][0] if jobs else None
        done = jobs.pop(0)[1](after) if jobs else half_sq
        if kind == "left" and bits:
            half_sq, done = lax.optimization_barrier((half_sq, done))
            for bit in bits[:2]:
                half_sq = exchange(half_sq, "dp", bit)
            bits = bits[2:]
        if step < owners - 1:
            down, up, half_sq, _ = lax.optimization_barrier((down, up, half_sq, done))
        downs.append(down)
        ups.append(up)
    while jobs:
        jobs.pop(0)[1]((downs[-1], ups[-1]))
    while bits:
        half_sq = exchange(half_sq, "dp", bits.pop(0))
    for block in rest:
        half_sq = half_sq + rest[block][2]
    while core_bits:
        half_sq = exchange(half_sq, "mp", core_bits.pop(0))
    rescale = lax.rsqrt(half_sq / (row_blocks * BLK * half_width * halves) + 1.0)

    pieces = []
    for block in rest:
        pieces += rest[block][:2]
    for down, up in zip(downs, ups):
        pieces += [down, up]
    canvas = None
    limit = 20
    shape = (row_blocks * BLK, half_width)
    early = len(pieces) - late_count
    cuts = [*range(0, early, limit), early, len(pieces)]
    for low, high in zip(cuts[:-1], cuts[1:]):
        group = pieces[low:high]
        canvas = place_pieces(canvas, shape, spots, low, rescale, group)
    return canvas, roots[0][None]


def solution(mesh):
    placed = (
        P(("member", "dp"), None),
        P(("member", "dp"), "mp"),
        P(("member", "mp"), None),
        P(("member", "mp"), None),
        P(("member", "mp"), None),
    )
    return jax.shard_map(
        shampoo_step,
        mesh=mesh,
        in_specs=placed,
        out_specs=(P("member", "mp"), P(("member", "mp"), "dp", None, None, None)),
        check_vma=False,
    )
```

profile of v0, /device:TPU:2, one launch (start us, length us, event | category | flops | bytes accessed | tf_op | source)
XLA Modules:
  0.0 351.3 jit_solution(18155388467521916328)
XLA Ops:
  1.9 1.6 collective-permute-start.3
  4.0 1.4 fusion.9
  5.4 1.6 collective-permute-start.2
  10.6 1.3 gather_fusion
  11.9 1.3 gather_fusion.1
  16.4 5.0 %collective-permute-done.2.refs_5_ = bf16[64,5120]{1,0:T(8,128)(2,1)S(1)} collective-permute-done((bf16[64,5120]{1,0:T(8,128)(2,1)S(1)}, bf16[64,5120]{1,0:T(8,128)(2,1)S(1)}, u32[]{:S(2)}, u32[]{:S(2)}) %collective-permute-start.2) | collective-permute-done | bytes 655392 | tf_op jit(solution)/shard_map/ppermute | solution.py:377
  23.1 1.5 collective-permute-start.6
  25.3 1.5 collective-permute-start.7
  29.6 10.5 %collective-permute-done.5.refs_21_ = bf16[512,128]{1,0:T(8,128)(2,1)S(1)} collective-permute-done((bf16[512,128]{1,0:T(8,128)(2,1)}, bf16[512,128]{1,0:T(8,128)(2,1)S(1)}, u32[]{:S(2)}, u32[]{:S(2)}) %collective-permute-start.5) | collective-permute-done | bytes 131104 | tf_op jit(solution)/shard_map/ppermute | solution.py:376
  40.7 1.6 collective-permute-start.8
  42.7 1.6 collective-permute-start.9
  44.8 12.6 %collective-permute-done.9.refs_23_ = bf16[512,128]{1,0:T(8,128)(2,1)S(1)} collective-permute-done((bf16[512,128]{1,0:T(8,128)(2,1)S(1)}, bf16[512,128]{1,0:T(8,128)(2,1)S(1)}, u32[]{:S(2)}, u32[]{:S(2)}) %collective-permute-start.9) | collective-permute-done | bytes 131104 | tf_op jit(solution)/shard_map/ppermute | solution.py:376
  57.3 1.3 collective-permute-done.11.refs_24_
  58.7 1.8 collective-permute-start.12
  60.7 1.7 collective-permute-start.13
  62.8 12.7 %collective-permute-done.13.refs_25_ = bf16[512,128]{1,0:T(8,128)(2,1)S(1)} collective-permute-done((bf16[512,128]{1,0:T(8,128)(2,1)S(1)}, bf16[512,128]{1,0:T(8,128)(2,1)S(1)}, u32[]{:S(2)}, u32[]{:S(2)}) %collective-permute-start.13) | collective-permute-done | bytes 131104 | tf_op jit(solution)/shard_map/ppermute | solution.py:376
  75.5 1.5 collective-permute-done.15.refs_26_
  77.0 1.9 collective-permute-start.16
  79.1 1.8 collective-permute-start.17
  81.1 12.8 %collective-permute-done.17.refs_27_ = bf16[512,128]{1,0:T(8,128)(2,1)S(1)} collective-permute-done((bf16[512,128]{1,0:T(8,128)(2,1)S(1)}, bf16[512,128]{1,0:T(8,128)(2,1)S(1)}, u32[]{:S(2)}, u32[]{:S(2)}) %collective-permute-start.17) | collective-permute-done | bytes 131104 | tf_op jit(solution)/shard_map/ppermute | solution.py:376
  95.0 1.9 collective-permute-start.20
  97.0 1.8 collective-permute-start.21
  99.1 12.9 %collective-permute-done.21.refs_29_ = bf16[512,128]{1,0:T(8,128)(2,1)} collective-permute-done((bf16[512,128]{1,0:T(8,128)(2,1)S(1)}, bf16[512,128]{1,0:T(8,128)(2,1)}, u32[]{:S(2)}, u32[]{:S(2)}) %collective-permute-start.21) | collective-permute-done | bytes 131104 | tf_op jit(solution)/shard_map/ppermute | solution.py:376
  112.9 1.8 collective-permute-start.24
  117.2 1.8 collective-permute-start.25
  119.3 7.1 %collective-permute-done.25.refs_31_ = bf16[512,128]{1,0:T(8,128)(2,1)} collective-permute-done((bf16[512,128]{1,0:T(8,128)(2,1)}, bf16[512,128]{1,0:T(8,128)(2,1)}, u32[]{:S(2)}, u32[]{:S(2)}) %collective-permute-start.25) | collective-permute-done | bytes 131104 | tf_op jit(solution)/shard_map/ppermute | solution.py:376
  126.5 1.7 collective-permute-done.27.refs_32_
  134.2 31.1 %shard_map.113 = (bf16[512,1024]{1,0:T(8,128)(2,1)}, bf16[512,1024]{1,0:T(8,128)(2,1)}, f32[1,1]{1,0:T(1,128)}) custom-call(s32[20]{0:T(128)} %reshape.422.refs_0_, f32[10]{0:T(128)} %reshape.423.refs_1_, s32[16]{0:T(128)} %pad_add_fusion.6.refs_2_, bf16[128,5120]{1,0:T(8,128)(2,1)} %refs_3_.13, bf16[64,5120]{1,0:T(8,128)(2,1)} %copy-done.14, ...), custom_call_target="tpu_custom_call" | custom-call | flops 27917287424 | bytes 12582912 | tf_op jit(solution)/shard_map/pallas_call | solution.py:219
  168.3 14.5 %shard_map.114.refs_48_ = bf16[1024,1024]{1,0:T(8,128)(2,1)} custom-call(s32[20]{0:T(128)} %reshape.422.refs_0_, f32[10]{0:T(128)} %reshape.423.refs_1_, s32[16]{0:T(128)} %pad_add_fusion.6.refs_2_, bf16[128,5120]{1,0:T(8,128)(2,1)} %refs_3_.13, bf16[64,5120]{1,0:T(8,128)(2,1)} %copy-done.14, bf16[64,5120]{1,0:T(8,128)(2,1)} %copy-done.13, ...), custom_call_target="tpu_custom_call" | custom-call | flops 12884901888 | bytes 12582912 | tf_op jit(solution)/shard_map/pallas_call | solution.py:219
  182.8 7.1 %collective-permute-start.45 = (f32[1,1]{1,0:T(1,128)}, f32[1,1]{1,0:T(1,128)}, u32[]{:S(2)}, u32[]{:S(2)}) collective-permute-start(f32[1,1]{1,0:T(1,128)} %select_n.161), channel_id=1, source_target_pairs={{0,2},{2,0},{4,6},{6,4},{8,10},{10,8},{12,14},{14,12},{1,3},{3,1},... | collective-permute-start | bytes 20 | tf_op jit(solution)/shard_map/ppermute | solution.py:411
  190.6 1.4 collective-permute-start.46
  191.9 2.4 collective-permute-done.46
  195.0 2.5 collective-permute-start.48
  197.5 20.1 %shard_map.115 = (bf16[512,1024]{1,0:T(8,128)(2,1)}, bf16[512,1024]{1,0:T(8,128)(2,1)}, f32[1,1]{1,0:T(1,128)}) custom-call(s32[20]{0:T(128)} %reshape.422.refs_0_, f32[10]{0:T(128)} %reshape.423.refs_1_, s32[16]{0:T(128)} %pad_add_fusion.6.refs_2_, bf16[128,5120]{1,0:T(8,128)(2,1)} %refs_3_.13, bf16[64,5120]{1,0:T(8,128)(2,1)} %copy-done.14, ...), custom_call_target="tpu_custom_call" | custom-call | flops 17179869184 | bytes 12582912 | tf_op jit(solution)/shard_map/pallas_call | solution.py:219
  218.1 1.7 collective-permute-start.49
  220.5 14.7 %shard_map.116.refs_48_ = bf16[1024,1024]{1,0:T(8,128)(2,1)} custom-call(s32[20]{0:T(128)} %reshape.422.refs_0_, f32[10]{0:T(128)} %reshape.423.refs_1_, s32[16]{0:T(128)} %pad_add_fusion.6.refs_2_, bf16[128,5120]{1,0:T(8,128)(2,1)} %refs_3_.13, bf16[64,5120]{1,0:T(8,128)(2,1)} %copy-done.14, bf16[64,5120]{1,0:T(8,128)(2,1)} %copy-done.13, ...), custom_call_target="tpu_custom_call" | custom-call | flops 12884901888 | bytes 12582912 | tf_op jit(solution)/shard_map/pallas_call | solution.py:219
  235.1 6.0 %collective-permute-start.51 = (f32[1,1]{1,0:T(1,128)}, f32[1,1]{1,0:T(1,128)}, u32[]{:S(2)}, u32[]{:S(2)}) collective-permute-start(f32[1,1]{1,0:T(1,128)} %add.169), channel_id=1, source_target_pairs={{0,8},{2,10},{4,12},{6,14},{8,0},{10,2},{12,4},{14,6},{1,9},{3,11}... | collective-permute-start | bytes 20 | tf_op jit(solution)/shard_map/ppermute | solution.py:411
  241.1 3.1 collective-permute-done.51
  245.5 1.4 collective-permute-start.53
  246.9 20.3 %shard_map.117 = (bf16[512,1024]{1,0:T(8,128)(2,1)}, bf16[512,1024]{1,0:T(8,128)(2,1)}, f32[1,1]{1,0:T(1,128)}) custom-call(s32[20]{0:T(128)} %reshape.422.refs_0_, f32[10]{0:T(128)} %reshape.423.refs_1_, s32[16]{0:T(128)} %pad_add_fusion.6.refs_2_, bf16[128,5120]{1,0:T(8,128)(2,1)} %refs_3_.13, bf16[64,5120]{1,0:T(8,128)(2,1)} %copy-done.14, ...), custom_call_target="tpu_custom_call" | custom-call | flops 17179869184 | bytes 12582912 | tf_op jit(solution)/shard_map/pallas_call | solution.py:219
  268.3 1.7 collective-permute-start.55
  270.0 26.2 %shard_map.118.refs_48_ = bf16[2,2,1024,1024]{3,2,1,0:T(8,128)(2,1)} custom-call(s32[20]{0:T(128)} %reshape.422.refs_0_, f32[10]{0:T(128)} %reshape.423.refs_1_, s32[16]{0:T(128)} %pad_add_fusion.6.refs_2_, bf16[128,5120]{1,0:T(8,128)(2,1)} %refs_3_.13, bf16[64,5120]{1,0:T(8,128)(2,1)} %copy-done.14, bf16[64,5120]{1,0:T(8,128)(2,1)} %copy-done.13, ...), custom_call_target="tpu_custom_call" | custom-call | flops 23622320128 | bytes 12582912 | tf_op jit(solution)/shard_map/pallas_call | solution.py:219
  296.3 2.2 collective-permute-start.57
  298.5 26.2 %shard_map.119 = bf16[2,2,1024,1024]{3,2,1,0:T(8,128)(2,1)} custom-call(s32[20]{0:T(128)} %reshape.422.refs_0_, f32[10]{0:T(128)} %reshape.423.refs_1_, s32[16]{0:T(128)} %pad_add_fusion.6.refs_2_, bf16[128,5120]{1,0:T(8,128)(2,1)} %refs_3_.13, bf16[64,5120]{1,0:T(8,128)(2,1)} %copy-done.14, ...), custom_call_target="tpu_custom_call", output_to_operand_aliasing={{}: (48, {})} | custom-call | flops 23622320128 | bytes 12582912 | tf_op jit(solution)/shard_map/pallas_call | solution.py:219
  324.9 2.2 collective-permute-start.60
  330.4 14.5 %place.2.refs_4_ = bf16[2048,5120]{1,0:T(8,128)(2,1)} custom-call(s32[40]{0:T(128)} %reshape.424.refs_0_, f32[1,1]{1,0:T(1,128)S(6)} %rsqrt.3.refs_1_, bf16[512,1024]{1,0:T(8,128)(2,1)} %get-tuple-element.102.refs_2_, bf16[512,1024]{1,0:T(8,128)(2,1)} %get-tuple-element.122.refs_3_, bf16[512,1024]{1,0:T(8,128)(2,1)} %get-tuple-element.110.refs_4_, ...), custom_call_target="tpu_custom_call" | custom-call | flops 1887436800 | bytes 37748736 | tf_op jit(solution)/shard_map/place/pallas_call | solution.py:278
  344.9 1.6 collective-permute-done.59.refs_2_
  347.4 3.5 %place.3 = bf16[2048,5120]{1,0:T(8,128)(2,1)} custom-call(s32[40]{0:T(128)} %reshape.424.refs_0_, f32[1,1]{1,0:T(1,128)S(6)} %rsqrt.3.refs_1_, bf16[512,1024]{1,0:T(8,128)(2,1)} %copy-done.11, bf16[512,1024]{1,0:T(8,128)(2,1)} %collective-permute-done.60.refs_3_, bf16[2048,5120]{1,0:T(8,128)(2,1)} %place.2.refs_4_), custom_call_target="tpu_custom_call", output_to_operand_aliasing={{}: (4, {})} | custom-call | flops 209715200 | bytes 4194304 | tf_op jit(solution)/shard_map/place/pallas_call | solution.py:278
  (213 shorter events, 35.1 us)
Async XLA Ops:
  1.9 14.4 %collective-permute-start.3 = (bf16[512,128]{1,0:T(8,128)(2,1)S(1)}, bf16[512,128]{1,0:T(8,128)(2,1)}, u32[]{:S(2)}, u32[]{:S(2)}) collective-permute-start(bf16[512,128]{1,0:T(8,128)(2,1)S(1)} %get-tuple-element.130), channel_id=1, source_target_pairs={{4,0},{8,4},{12,8},{14,12},{10,14},{6,10},{2,6},{0,2},{5,1},{9,5},... | collective-permute-start | bytes 393224 | tf_op jit(solution)/shard_map/ppermute | solution.py:377
  3.5 12.9 %collective-permute-start.1 = (bf16[512,128]{1,0:T(8,128)(2,1)S(1)}, bf16[512,128]{1,0:T(8,128)(2,1)}, u32[]{:S(2)}, u32[]{:S(2)}) collective-permute-start(bf16[512,128]{1,0:T(8,128)(2,1)S(1)} %get-tuple-element.131), channel_id=1, source_target_pairs={{0,4},{4,8},{8,12},{12,14},{14,10},{10,6},{6,2},{2,0},{1,5},{5,9},... | collective-permute-start | bytes 393224 | tf_op jit(solution)/shard_map/ppermute | solution.py:376
  5.4 16.0 %collective-permute-start.2 = (bf16[64,5120]{1,0:T(8,128)(2,1)S(1)}, bf16[64,5120]{1,0:T(8,128)(2,1)S(1)}, u32[]{:S(2)}, u32[]{:S(2)}) collective-permute-start(bf16[64,5120]{1,0:T(8,128)(2,1)S(1)} %get-tuple-element.128), channel_id=1, source_target_pairs={{4,0},{8,4},{12,8},{14,12},{10,14},{6,10},{2,6},{0,2},{5,1},{9,5},... | collective-permute-start | bytes 1966088 | tf_op jit(solution)/shard_map/ppermute | solution.py:377
  6.9 15.6 %collective-permute-start = (bf16[64,5120]{1,0:T(8,128)(2,1)S(1)}, bf16[64,5120]{1,0:T(8,128)(2,1)S(1)}, u32[]{:S(2)}, u32[]{:S(2)}) collective-permute-start(bf16[64,5120]{1,0:T(8,128)(2,1)S(1)} %get-tuple-element.129), channel_id=1, source_target_pairs={{0,4},{4,8},{8,12},{12,14},{14,10},{10,6},{6,2},{2,0},{1,5},{5,9},... | collective-permute-start | bytes 1966088 | tf_op jit(solution)/shard_map/ppermute | solution.py:376
  22.6 18.1 %collective-permute-start.4 = (bf16[64,5120]{1,0:T(8,128)(2,1)S(1)}, bf16[64,5120]{1,0:T(8,128)(2,1)S(1)}, u32[]{:S(2)}, u32[]{:S(2)}) collective-permute-start(bf16[64,5120]{1,0:T(8,128)(2,1)S(1)} %collective-permute-done.refs_4_), channel_id=1, source_target_pairs={{0,4},{4,8},{8,12},{12,14},{14,10},{10,6},{6,2},{2,0},{1,5},{5,9},... | collective-permute-start | bytes 1966088 | tf_op jit(solution)/shard_map/ppermute | solution.py:376
  23.1 17.6 %collective-permute-start.6 = (bf16[64,5120]{1,0:T(8,128)(2,1)S(1)}, bf16[64,5120]{1,0:T(8,128)(2,1)S(1)}, u32[]{:S(2)}, u32[]{:S(2)}) collective-permute-start(bf16[64,5120]{1,0:T(8,128)(2,1)S(1)} %collective-permute-done.2.refs_5_), channel_id=1, source_target_pairs={{4,0},{8,4},{12,8},{14,12},{10,14},{6,10},{2,6},{0,2},{5,1},{9,5},... | collective-permute-start | bytes 1966088 | tf_op jit(solution)/shard_map/ppermute | solution.py:377
  24.8 15.4 %collective-permute-start.5 = (bf16[512,128]{1,0:T(8,128)(2,1)}, bf16[512,128]{1,0:T(8,128)(2,1)S(1)}, u32[]{:S(2)}, u32[]{:S(2)}) collective-permute-start(bf16[512,128]{1,0:T(8,128)(2,1)} %collective-permute-done.1.refs_19_), channel_id=1, source_target_pairs={{0,4},{4,8},{8,12},{12,14},{14,10},{10,6},{6,2},{2,0},{1,5},{5,9},... | collective-permute-start | bytes 393224 | tf_op jit(solution)/shard_map/ppermute | solution.py:376
  25.3 15.3 %collective-permute-start.7 = (bf16[512,128]{1,0:T(8,128)(2,1)}, bf16[512,128]{1,0:T(8,128)(2,1)}, u32[]{:S(2)}, u32[]{:S(2)}) collective-permute-start(bf16[512,128]{1,0:T(8,128)(2,1)} %collective-permute-done.3.refs_20_), channel_id=1, source_target_pairs={{4,0},{8,4},{12,8},{14,12},{10,14},{6,10},{2,6},{0,2},{5,1},{9,5},... | collective-permute-start | bytes 393224 | tf_op jit(solution)/shard_map/ppermute | solution.py:377
  40.7 18.0 %collective-permute-start.8 = (bf16[64,5120]{1,0:T(8,128)(2,1)S(1)}, bf16[64,5120]{1,0:T(8,128)(2,1)S(1)}, u32[]{:S(2)}, u32[]{:S(2)}) collective-permute-start(bf16[64,5120]{1,0:T(8,128)(2,1)S(1)} %collective-permute-done.4.refs_6_), channel_id=1, source_target_pairs={{0,4},{4,8},{8,12},{12,14},{14,10},{10,6},{6,2},{2,0},{1,5},{5,9},... | collective-permute-start | bytes 1966088 | tf_op jit(solution)/shard_map/ppermute | solution.py:376
  42.3 16.3 %collective-permute-start.10 = (bf16[64,5120]{1,0:T(8,128)(2,1)S(1)}, bf16[64,5120]{1,0:T(8,128)(2,1)S(1)}, u32[]{:S(2)}, u32[]{:S(2)}) collective-permute-start(bf16[64,5120]{1,0:T(8,128)(2,1)S(1)} %collective-permute-done.6.refs_7_), channel_id=1, source_target_pairs={{4,0},{8,4},{12,8},{14,12},{10,14},{6,10},{2,6},{0,2},{5,1},{9,5},... | collective-permute-start | bytes 1966088 | tf_op jit(solution)/shard_map/ppermute | solution.py:377
  42.7 14.6 %collective-permute-start.9 = (bf16[512,128]{1,0:T(8,128)(2,1)S(1)}, bf16[512,128]{1,0:T(8,128)(2,1)S(1)}, u32[]{:S(2)}, u32[]{:S(2)}) collective-permute-start(bf16[512,128]{1,0:T(8,128)(2,1)S(1)} %collective-permute-done.5.refs_21_), channel_id=1, source_target_pairs={{0,4},{4,8},{8,12},{12,14},{14,10},{10,6},{6,2},{2,0},{1,5},{5,9},... | collective-permute-start | bytes 393224 | tf_op jit(solution)/shard_map/ppermute | solution.py:376
  44.3 14.3 %collective-permute-start.11 = (bf16[512,128]{1,0:T(8,128)(2,1)}, bf16[512,128]{1,0:T(8,128)(2,1)S(1)}, u32[]{:S(2)}, u32[]{:S(2)}) collective-permute-start(bf16[512,128]{1,0:T(8,128)(2,1)} %collective-permute-done.7.refs_22_), channel_id=1, source_target_pairs={{4,0},{8,4},{12,8},{14,12},{10,14},{6,10},{2,6},{0,2},{5,1},{9,5},... | collective-permute-start | bytes 393224 | tf_op jit(solution)/shard_map/ppermute | solution.py:377
  58.7 18.3 %collective-permute-start.12 = (bf16[64,5120]{1,0:T(8,128)(2,1)S(1)}, bf16[64,5120]{1,0:T(8,128)(2,1)S(1)}, u32[]{:S(2)}, u32[]{:S(2)}) collective-permute-start(bf16[64,5120]{1,0:T(8,128)(2,1)S(1)} %collective-permute-done.8.refs_8_), channel_id=1, source_target_pairs={{0,4},{4,8},{8,12},{12,14},{14,10},{10,6},{6,2},{2,0},{1,5},{5,9},... | collective-permute-start | bytes 1966088 | tf_op jit(solution)/shard_map/ppermute | solution.py:376
  60.5 16.5 %collective-permute-start.14 = (bf16[64,5120]{1,0:T(8,128)(2,1)S(1)}, bf16[64,5120]{1,0:T(8,128)(2,1)S(1)}, u32[]{:S(2)}, u32[]{:S(2)}) collective-permute-start(bf16[64,5120]{1,0:T(8,128)(2,1)S(1)} %collective-permute-done.10.refs_9_), channel_id=1, source_target_pairs={{4,0},{8,4},{12,8},{14,12},{10,14},{6,10},{2,6},{0,2},{5,1},{9,5},... | collective-permute-start | bytes 1966088 | tf_op jit(solution)/shard_map/ppermute | solution.py:377
  60.7 14.7 %collective-permute-start.13 = (bf16[512,128]{1,0:T(8,128)(2,1)S(1)}, bf16[512,128]{1,0:T(8,128)(2,1)S(1)}, u32[]{:S(2)}, u32[]{:S(2)}) collective-permute-start(bf16[512,128]{1,0:T(8,128)(2,1)S(1)} %collective-permute-done.9.refs_23_), channel_id=1, source_target_pairs={{0,4},{4,8},{8,12},{12,14},{14,10},{10,6},{6,2},{2,0},{1,5},{5,9},... | collective-permute-start | bytes 393224 | tf_op jit(solution)/shard_map/ppermute | solution.py:376
  62.5 14.5 %collective-permute-start.15 = (bf16[512,128]{1,0:T(8,128)(2,1)S(1)}, bf16[512,128]{1,0:T(8,128)(2,1)S(1)}, u32[]{:S(2)}, u32[]{:S(2)}) collective-permute-start(bf16[512,128]{1,0:T(8,128)(2,1)S(1)} %collective-permute-done.11.refs_24_), channel_id=1, source_target_pairs={{4,0},{8,4},{12,8},{14,12},{10,14},{6,10},{2,6},{0,2},{5,1},{9,5},... | collective-permute-start | bytes 393224 | tf_op jit(solution)/shard_map/ppermute | solution.py:377
  77.0 17.9 %collective-permute-start.16 = (bf16[64,5120]{1,0:T(8,128)(2,1)S(1)}, bf16[64,5120]{1,0:T(8,128)(2,1)S(1)}, u32[]{:S(2)}, u32[]{:S(2)}) collective-permute-start(bf16[64,5120]{1,0:T(8,128)(2,1)S(1)} %collective-permute-done.12.refs_10_), channel_id=1, source_target_pairs={{0,4},{4,8},{8,12},{12,14},{14,10},{10,6},{6,2},{2,0},{1,5},{5,9},... | collective-permute-start | bytes 1966088 | tf_op jit(solution)/shard_map/ppermute | solution.py:376
  78.9 16.1 %collective-permute-start.18 = (bf16[64,5120]{1,0:T(8,128)(2,1)S(1)}, bf16[64,5120]{1,0:T(8,128)(2,1)S(1)}, u32[]{:S(2)}, u32[]{:S(2)}) collective-permute-start(bf16[64,5120]{1,0:T(8,128)(2,1)S(1)} %collective-permute-done.14.refs_11_), channel_id=1, source_target_pairs={{4,0},{8,4},{12,8},{14,12},{10,14},{6,10},{2,6},{0,2},{5,1},{9,5},... | collective-permute-start | bytes 1966088 | tf_op jit(solution)/shard_map/ppermute | solution.py:377
  79.1 14.9 %collective-permute-start.17 = (bf16[512,128]{1,0:T(8,128)(2,1)S(1)}, bf16[512,128]{1,0:T(8,128)(2,1)S(1)}, u32[]{:S(2)}, u32[]{:S(2)}) collective-permute-start(bf16[512,128]{1,0:T(8,128)(2,1)S(1)} %collective-permute-done.13.refs_25_), channel_id=1, source_target_pairs={{0,4},{4,8},{8,12},{12,14},{14,10},{10,6},{6,2},{2,0},{1,5},{5,9},... | collective-permute-start | bytes 393224 | tf_op jit(solution)/shard_map/ppermute | solution.py:376
  80.9 14.0 %collective-permute-start.19 = (bf16[512,128]{1,0:T(8,128)(2,1)S(1)}, bf16[512,128]{1,0:T(8,128)(2,1)}, u32[]{:S(2)}, u32[]{:S(2)}) collective-permute-start(bf16[512,128]{1,0:T(8,128)(2,1)S(1)} %collective-permute-done.15.refs_26_), channel_id=1, source_target_pairs={{4,0},{8,4},{12,8},{14,12},{10,14},{6,10},{2,6},{0,2},{5,1},{9,5},... | collective-permute-start | bytes 393224 | tf_op jit(solution)/shard_map/ppermute | solution.py:377
  95.0 17.9 %collective-permute-start.20 = (bf16[64,5120]{1,0:T(8,128)(2,1)S(1)}, bf16[64,5120]{1,0:T(8,128)(2,1)S(1)}, u32[]{:S(2)}, u32[]{:S(2)}) collective-permute-start(bf16[64,5120]{1,0:T(8,128)(2,1)S(1)} %collective-permute-done.16.refs_12_), channel_id=1, source_target_pairs={{0,4},{4,8},{8,12},{12,14},{14,10},{10,6},{6,2},{2,0},{1,5},{5,9},... | collective-permute-start | bytes 1966088 | tf_op jit(solution)/shard_map/ppermute | solution.py:376
  96.8 16.1 %collective-permute-start.22 = (bf16[64,5120]{1,0:T(8,128)(2,1)S(1)}, bf16[64,5120]{1,0:T(8,128)(2,1)S(1)}, u32[]{:S(2)}, u32[]{:S(2)}) collective-permute-start(bf16[64,5120]{1,0:T(8,128)(2,1)S(1)} %collective-permute-done.18.refs_13_), channel_id=1, source_target_pairs={{4,0},{8,4},{12,8},{14,12},{10,14},{6,10},{2,6},{0,2},{5,1},{9,5},... | collective-permute-start | bytes 1966088 | tf_op jit(solution)/shard_map/ppermute | solution.py:377
  97.0 14.9 %collective-permute-start.21 = (bf16[512,128]{1,0:T(8,128)(2,1)S(1)}, bf16[512,128]{1,0:T(8,128)(2,1)}, u32[]{:S(2)}, u32[]{:S(2)}) collective-permute-start(bf16[512,128]{1,0:T(8,128)(2,1)S(1)} %collective-permute-done.17.refs_27_), channel_id=1, source_target_pairs={{0,4},{4,8},{8,12},{12,14},{14,10},{10,6},{6,2},{2,0},{1,5},{5,9},... | collective-permute-start | bytes 393224 | tf_op jit(solution)/shard_map/ppermute | solution.py:376
  98.9 14.0 %collective-permute-start.23 = (bf16[512,128]{1,0:T(8,128)(2,1)}, bf16[512,128]{1,0:T(8,128)(2,1)}, u32[]{:S(2)}, u32[]{:S(2)}) collective-permute-start(bf16[512,128]{1,0:T(8,128)(2,1)} %collective-permute-done.19.refs_28_), channel_id=1, source_target_pairs={{4,0},{8,4},{12,8},{14,12},{10,14},{6,10},{2,6},{0,2},{5,1},{9,5},... | collective-permute-start | bytes 393224 | tf_op jit(solution)/shard_map/ppermute | solution.py:377
  112.9 15.3 %collective-permute-start.24 = (bf16[64,5120]{1,0:T(8,128)(2,1)S(1)}, bf16[64,5120]{1,0:T(8,128)(2,1)S(1)}, u32[]{:S(2)}, u32[]{:S(2)}) collective-permute-start(bf16[64,5120]{1,0:T(8,128)(2,1)S(1)} %collective-permute-done.20.refs_14_), channel_id=1, source_target_pairs={{0,4},{4,8},{8,12},{12,14},{14,10},{10,6},{6,2},{2,0},{1,5},{5,9},... | collective-permute-start | bytes 1966088 | tf_op jit(solution)/shard_map/ppermute | solution.py:376
  114.7 14.1 %collective-permute-start.26 = (bf16[64,5120]{1,0:T(8,128)(2,1)S(1)}, bf16[64,5120]{1,0:T(8,128)(2,1)S(1)}, u32[]{:S(2)}, u32[]{:S(2)}) collective-permute-start(bf16[64,5120]{1,0:T(8,128)(2,1)S(1)} %collective-permute-done.22.refs_15_), channel_id=1, source_target_pairs={{4,0},{8,4},{12,8},{14,12},{10,14},{6,10},{2,6},{0,2},{5,1},{9,5},... | collective-permute-start | bytes 1966088 | tf_op jit(solution)/shard_map/ppermute | solution.py:377
  117.2 9.3 %collective-permute-start.25 = (bf16[512,128]{1,0:T(8,128)(2,1)}, bf16[512,128]{1,0:T(8,128)(2,1)}, u32[]{:S(2)}, u32[]{:S(2)}) collective-permute-start(bf16[512,128]{1,0:T(8,128)(2,1)} %collective-permute-done.21.refs_29_), channel_id=1, source_target_pairs={{0,4},{4,8},{8,12},{12,14},{14,10},{10,6},{6,2},{2,0},{1,5},{5,9},... | collective-permute-start | bytes 393224 | tf_op jit(solution)/shard_map/ppermute | solution.py:376
  118.9 9.2 %collective-permute-start.27 = (bf16[512,128]{1,0:T(8,128)(2,1)}, bf16[512,128]{1,0:T(8,128)(2,1)}, u32[]{:S(2)}, u32[]{:S(2)}) collective-permute-start(bf16[512,128]{1,0:T(8,128)(2,1)} %collective-permute-done.23.refs_30_), channel_id=1, source_target_pairs={{4,0},{8,4},{12,8},{14,12},{10,14},{6,10},{2,6},{0,2},{5,1},{9,5},... | collective-permute-start | bytes 393224 | tf_op jit(solution)/shard_map/ppermute | solution.py:377
  119.3 10.6 %collective-permute-start.33 = (bf16[512,128]{1,0:T(8,128)(2,1)S(1)}, bf16[512,128]{1,0:T(8,128)(2,1)S(1)}, u32[]{:S(2)}, u32[]{:S(2)}) collective-permute-start(bf16[512,128]{1,0:T(8,128)(2,1)S(1)} %collective-permute-done.9.refs_23_), channel_id=1, source_target_pairs={{0,1},{1,0},{2,3},{3,2},{4,5},{5,4},{6,7},{7,6},{8,9},{9,8},{10,11... | collective-permute-start | bytes 393224 | tf_op jit(solution)/shard_map/ppermute | solution.py:385
  126.5 4.0 %collective-permute-start.34 = (bf16[512,128]{1,0:T(8,128)(2,1)S(1)}, bf16[512,128]{1,0:T(8,128)(2,1)S(1)}, u32[]{:S(2)}, u32[]{:S(2)}) collective-permute-start(bf16[512,128]{1,0:T(8,128)(2,1)S(1)} %collective-permute-done.11.refs_24_), channel_id=1, source_target_pairs={{0,1},{1,0},{2,3},{3,2},{4,5},{5,4},{6,7},{7,6},{8,9},{9,8},{10,11... | collective-permute-start | bytes 393224 | tf_op jit(solution)/shard_map/ppermute | solution.py:385
  128.2 2.9 collective-permute-start.36
  165.3 29.6 %collective-permute-start.43 = (bf16[512,1024]{1,0:T(8,128)(2,1)}, bf16[512,1024]{1,0:T(8,128)(2,1)S(1)}, u32[]{:S(2)}, u32[]{:S(2)}) collective-permute-start(bf16[512,1024]{1,0:T(8,128)(2,1)} %get-tuple-element.95.refs_6_), channel_id=1, source_target_pairs={{0,4},{4,8},{8,12},{12,14},{14,10},{10,6},{6,2},{2,0},{1,5},{5,9},... | collective-permute-start | bytes 3145736 | tf_op jit(solution)/shard_map/ppermute | solution.py:418
  166.5 28.4 %collective-permute-start.44 = (bf16[512,1024]{1,0:T(8,128)(2,1)}, bf16[512,1024]{1,0:T(8,128)(2,1)S(1)}, u32[]{:S(2)}, u32[]{:S(2)}) collective-permute-start(bf16[512,1024]{1,0:T(8,128)(2,1)} %get-tuple-element.96.refs_7_), channel_id=1, source_target_pairs={{4,0},{8,4},{12,8},{14,12},{10,14},{6,10},{2,6},{0,2},{5,1},{9,5},... | collective-permute-start | bytes 3145736 | tf_op jit(solution)/shard_map/ppermute | solution.py:419
  182.8 7.1 %collective-permute-start.45 = (f32[1,1]{1,0:T(1,128)}, f32[1,1]{1,0:T(1,128)}, u32[]{:S(2)}, u32[]{:S(2)}) collective-permute-start(f32[1,1]{1,0:T(1,128)} %select_n.161), channel_id=1, source_target_pairs={{0,2},{2,0},{4,6},{6,4},{8,10},{10,8},{12,14},{14,12},{1,3},{3,1},... | collective-permute-start | bytes 20 | tf_op jit(solution)/shard_map/ppermute | solution.py:411
  190.6 3.7 %collective-permute-start.46 = (f32[1,1]{1,0:T(1,128)}, f32[1,1]{1,0:T(1,128)}, u32[]{:S(2)}, u32[]{:S(2)}) collective-permute-start(f32[1,1]{1,0:T(1,128)} %add.168), channel_id=1, source_target_pairs={{0,4},{2,6},{4,0},{6,2},{8,12},{10,14},{12,8},{14,10},{1,5},{3,7},... | collective-permute-start | bytes 20 | tf_op jit(solution)/shard_map/ppermute | solution.py:411
  194.9 23.2 %collective-permute-start.47 = (bf16[512,1024]{1,0:T(8,128)(2,1)S(1)}, bf16[512,1024]{1,0:T(8,128)(2,1)S(1)}, u32[]{:S(2)}, u32[]{:S(2)}) collective-permute-start(bf16[512,1024]{1,0:T(8,128)(2,1)S(1)} %collective-permute-done.43.refs_49_.refs_8_), channel_id=1, source_target_pairs={{0,4},{4,8},{8,12},{12,14},{14,10},{10,6},{6,2},{2,0},{1,5},{5,9},... | collective-permute-start | bytes 3145736 | tf_op jit(solution)/shard_map/ppermute | solution.py:418
  195.0 23.1 %collective-permute-start.48 = (bf16[512,1024]{1,0:T(8,128)(2,1)S(1)}, bf16[512,1024]{1,0:T(8,128)(2,1)}, u32[]{:S(2)}, u32[]{:S(2)}) collective-permute-start(bf16[512,1024]{1,0:T(8,128)(2,1)S(1)} %collective-permute-done.44.refs_50_.refs_9_), channel_id=1, source_target_pairs={{4,0},{8,4},{12,8},{14,12},{10,14},{6,10},{2,6},{0,2},{5,1},{9,5},... | collective-permute-start | bytes 3145736 | tf_op jit(solution)/shard_map/ppermute | solution.py:419
  218.1 26.7 %collective-permute-start.49 = (bf16[512,1024]{1,0:T(8,128)(2,1)S(1)}, bf16[512,1024]{1,0:T(8,128)(2,1)S(1)}, u32[]{:S(2)}, u32[]{:S(2)}) collective-permute-start(bf16[512,1024]{1,0:T(8,128)(2,1)S(1)} %collective-permute-done.47.refs_48_.refs_10_), channel_id=1, source_target_pairs={{0,4},{4,8},{8,12},{12,14},{14,10},{10,6},{6,2},{2,0},{1,5},{5,9},... | collective-permute-start | bytes 3145736 | tf_op jit(solution)/shard_map/ppermute | solution.py:418
  219.8 25.1 %collective-permute-start.50 = (bf16[512,1024]{1,0:T(8,128)(2,1)}, bf16[512,1024]{1,0:T(8,128)(2,1)S(1)}, u32[]{:S(2)}, u32[]{:S(2)}) collective-permute-start(bf16[512,1024]{1,0:T(8,128)(2,1)} %collective-permute-done.48.refs_49_.refs_11_), channel_id=1, source_target_pairs={{4,0},{8,4},{12,8},{14,12},{10,14},{6,10},{2,6},{0,2},{5,1},{9,5},... | collective-permute-start | bytes 3145736 | tf_op jit(solution)/shard_map/ppermute | solution.py:419
  235.1 9.0 %collective-permute-start.51 = (f32[1,1]{1,0:T(1,128)}, f32[1,1]{1,0:T(1,128)}, u32[]{:S(2)}, u32[]{:S(2)}) collective-permute-start(f32[1,1]{1,0:T(1,128)} %add.169), channel_id=1, source_target_pairs={{0,8},{2,10},{4,12},{6,14},{8,0},{10,2},{12,4},{14,6},{1,9},{3,11}... | collective-permute-start | bytes 20 | tf_op jit(solution)/shard_map/ppermute | solution.py:411
  244.9 22.4 %collective-permute-start.52 = (bf16[512,1024]{1,0:T(8,128)(2,1)S(1)}, bf16[512,1024]{1,0:T(8,128)(2,1)S(1)}, u32[]{:S(2)}, u32[]{:S(2)}) collective-permute-start(bf16[512,1024]{1,0:T(8,128)(2,1)S(1)} %collective-permute-done.49.refs_49_.refs_12_), channel_id=1, source_target_pairs={{0,4},{4,8},{8,12},{12,14},{14,10},{10,6},{6,2},{2,0},{1,5},{5,9},... | collective-permute-start | bytes 3145736 | tf_op jit(solution)/shard_map/ppermute | solution.py:418
  245.5 22.3 %collective-permute-start.53 = (bf16[512,1024]{1,0:T(8,128)(2,1)S(1)}, bf16[512,1024]{1,0:T(8,128)(2,1)}, u32[]{:S(2)}, u32[]{:S(2)}) collective-permute-start(bf16[512,1024]{1,0:T(8,128)(2,1)S(1)} %collective-permute-done.50.refs_50_.refs_13_), channel_id=1, source_target_pairs={{4,0},{8,4},{12,8},{14,12},{10,14},{6,10},{2,6},{0,2},{5,1},{9,5},... | collective-permute-start | bytes 3145736 | tf_op jit(solution)/shard_map/ppermute | solution.py:419
  267.8 28.4 %collective-permute-start.54 = (bf16[512,1024]{1,0:T(8,128)(2,1)S(1)}, bf16[512,1024]{1,0:T(8,128)(2,1)S(1)}, u32[]{:S(2)}, u32[]{:S(2)}) collective-permute-start(bf16[512,1024]{1,0:T(8,128)(2,1)S(1)} %collective-permute-done.52.refs_48_.refs_14_), channel_id=1, source_target_pairs={{0,4},{4,8},{8,12},{12,14},{14,10},{10,6},{6,2},{2,0},{1,5},{5,9},... | collective-permute-start | bytes 3145736 | tf_op jit(solution)/shard_map/ppermute | solution.py:418
  268.3 27.9 %collective-permute-start.55 = (bf16[512,1024]{1,0:T(8,128)(2,1)}, bf16[512,1024]{1,0:T(8,128)(2,1)S(1)}, u32[]{:S(2)}, u32[]{:S(2)}) collective-permute-start(bf16[512,1024]{1,0:T(8,128)(2,1)} %collective-permute-done.53.refs_49_.refs_15_), channel_id=1, source_target_pairs={{4,0},{8,4},{12,8},{14,12},{10,14},{6,10},{2,6},{0,2},{5,1},{9,5},... | collective-permute-start | bytes 3145736 | tf_op jit(solution)/shard_map/ppermute | solution.py:419
  296.3 28.5 %collective-permute-start.56 = (bf16[512,1024]{1,0:T(8,128)(2,1)S(1)}, bf16[512,1024]{1,0:T(8,128)(2,1)S(1)}, u32[]{:S(2)}, u32[]{:S(2)}) collective-permute-start(bf16[512,1024]{1,0:T(8,128)(2,1)S(1)} %collective-permute-done.54.refs_49_.refs_16_), channel_id=1, source_target_pairs={{0,4},{4,8},{8,12},{12,14},{14,10},{10,6},{6,2},{2,0},{1,5},{5,9},... | collective-permute-start | bytes 3145736 | tf_op jit(solution)/shard_map/ppermute | solution.py:418
  296.3 28.4 %collective-permute-start.57 = (bf16[512,1024]{1,0:T(8,128)(2,1)S(1)}, bf16[512,1024]{1,0:T(8,128)(2,1)}, u32[]{:S(2)}, u32[]{:S(2)}) collective-permute-start(bf16[512,1024]{1,0:T(8,128)(2,1)S(1)} %collective-permute-done.55.refs_50_.refs_17_), channel_id=1, source_target_pairs={{4,0},{8,4},{12,8},{14,12},{10,14},{6,10},{2,6},{0,2},{5,1},{9,5},... | collective-permute-start | bytes 3145736 | tf_op jit(solution)/shard_map/ppermute | solution.py:419
  324.8 21.7 %collective-permute-start.59 = (bf16[512,1024]{1,0:T(8,128)(2,1)S(1)}, bf16[512,1024]{1,0:T(8,128)(2,1)S(1)}, u32[]{:S(2)}, u32[]{:S(2)}) collective-permute-start(bf16[512,1024]{1,0:T(8,128)(2,1)S(1)} %collective-permute-done.56.refs_18_), channel_id=1, source_target_pairs={{0,4},{4,8},{8,12},{12,14},{14,10},{10,6},{6,2},{2,0},{1,5},{5,9},... | collective-permute-start | bytes 3145736 | tf_op jit(solution)/shard_map/ppermute | solution.py:418
  324.9 22.6 %collective-permute-start.60 = (bf16[512,1024]{1,0:T(8,128)(2,1)}, bf16[512,1024]{1,0:T(8,128)(2,1)}, u32[]{:S(2)}, u32[]{:S(2)}) collective-permute-start(bf16[512,1024]{1,0:T(8,128)(2,1)} %collective-permute-done.57.refs_19_), channel_id=1, source_target_pairs={{4,0},{8,4},{12,8},{14,12},{10,14},{6,10},{2,6},{0,2},{5,1},{9,5},... | collective-permute-start | bytes 3145736 | tf_op jit(solution)/shard_map/ppermute | solution.py:419
  (56 other events, 1327.0 us)
where the time goes:
time: 358 us; the launch traced here: 351 us
  Pallas kernels  171 us (48%)
  waiting for transfers between devices  93 us (26%)
  starting transfers between devices  64.1 us (18%)
  local copies, waits for them, and re-layouts  12.6 us (4%)
  between operations  5.8 us (2%)
  other arithmetic  4.65 us (1%)
    pallas_call x7, Pallas kernels, run_block(): pl.pallas_call(functools.partial(block_kernel, kind, owners, turns, len(a...  153 us
    ppermute x14, waiting for transfers between devices, shampoo_step(): down = tuple((lax.ppermute(piece, 'dp', ahead) for piece in down))  70 us
    ppermute x14, starting transfers between devices, shampoo_step(): down = tuple((lax.ppermute(piece, 'dp', ahead) for piece in down))  19.8 us
    pallas_call x2, Pallas kernels, place_pieces(): pl.pallas_call(functools.partial(place_kernel, first, count, len(old)), o...  18 us
    ppermute x4, starting transfers between devices, exchange(): return value + lax.ppermute(value, axis, pairs)  15.5 us
    ppermute x7, starting transfers between devices, shampoo_step(): up = lax.ppermute(ups[-1], 'dp', back)  12 us
    ppermute x14, waiting for transfers between devices, shampoo_step(): up = tuple((lax.ppermute(piece, 'dp', back) for piece in up))  11.9 us
    ppermute x14, starting transfers between devices, shampoo_step(): up = tuple((lax.ppermute(piece, 'dp', back) for piece in up))  9.11 us
  transfers between devices with their start and end apart: 61, of which 23 were waited for; matrix products, arithmetic and copies ran while one was open for 4% of the time, Pallas kernels for 39%

commit v1 on v0

--- a/solution.py
+++ b/solution.py
@@ -241,17 +241,19 @@
     )(*operands)
 
 
-def place_kernel(first, count, extra, *refs):
+def place_kernel(first, count, late_count, extra, *refs):
     spots, rescale = refs[:2]
     pieces = refs[2 : 2 + count]
     canvas, held, in_sems, out_sems = refs[2 + count + extra :]
+    near = late_count > 0
     rows = held.shape[1]
     loads = []
     stores = []
     for index in range(count):
         row = pl.multiple_of(spots[2 * (first + index)], rows)
         column = pl.multiple_of(spots[2 * (first + index) + 1], BLK)
-        loads.append(pltpu.make_async_copy(pieces[index], held.at[index], in_sems.at[index]))
+        if not near:
+            loads.append(pltpu.make_async_copy(pieces[index], held.at[index], in_sems.at[index]))
         stores.append(
             pltpu.make_async_copy(
                 held.at[index],
@@ -259,26 +261,30 @@
                 out_sems.at[index],
             )
         )
-    for load in loads:
-        load.start()
+    if not near:
+        for load in loads:
+            load.start()
     for index in range(count):
-        loads[index].wait()
-        wide = held[index].astype(jnp.float32) * rescale[0, 0]
+        if not near:
+            loads[index].wait()
+        piece = pieces[index] if near else held.at[index]
+        wide = piece[...].astype(jnp.float32) * rescale[0, 0]
         held[index] = wide.astype(jnp.bfloat16)
         stores[index].start()
     for store in stores:
         store.wait()
 
 
-def place_pieces(canvas, shape, spots, first, rescale, pieces):
+def place_pieces(canvas, shape, spots, first, rescale, pieces, late_count=0):
     count = len(pieces)
     smem = pl.BlockSpec(memory_space=pltpu.SMEM)
     hbm = pl.BlockSpec(memory_space=HBM)
+    vmem = pl.BlockSpec(memory_space=pltpu.VMEM)
     old = [] if canvas is None else [canvas]
     return pl.pallas_call(
-        functools.partial(place_kernel, first, count, len(old)),
+        functools.partial(place_kernel, first, count, late_count, len(old)),
         out_shape=jax.ShapeDtypeStruct(shape, jnp.bfloat16),
-        in_specs=[smem, smem] + [hbm] * (count + len(old)),
+        in_specs=[smem, smem] + [vmem if late_count else hbm] * count + [hbm] * len(old),
         out_specs=hbm,
         input_output_aliases={2 + count: 0} if old else {},
         scratch_shapes=[
@@ -299,6 +305,11 @@
     ahead = [(order[i], order[(i + 1) % count]) for i in range(count)]
     back = [(b, a) for a, b in ahead]
     return order, ahead, back
+
+
+def sum_steps(owners):
+    bits = [1 << i for i in range((owners - 1).bit_length())]
+    return dict(zip([0, 1, 3, 4, 2, *range(5, owners)], bits))
 
 
 def shampoo_step(activations, out_grads, slot_table, exponent_index, damping_index):
@@ -370,19 +381,22 @@
     act_chunks = [[act_part]]
     for shift in mp_shifts:
         act_chunks.append([lax.ppermute(act_part, "mp", shift)])
-    down = (out_grads[:half_tok], act_part[:half_row])
-    up = (out_grads[half_tok:], act_part[half_row:])
+    down, up = out_grads[:half_tok], out_grads[half_tok:]
+    acts = (act_part[:half_row], act_part[half_row:])
     for step in range(1, owners):
-        down = tuple(lax.ppermute(piece, "dp", ahead) for piece in down)
-        up = tuple(lax.ppermute(piece, "dp", back) for piece in up)
+        down = lax.ppermute(down, "dp", ahead)
+        up = lax.ppermute(up, "dp", back)
+        for act_step in (1, 2) if step == 1 else (step + 1,):
+            if act_step < owners:
+                acts = (lax.ppermute(acts[0], "dp", ahead), lax.ppermute(acts[1], "dp", back))
+                act_chunks[0] += acts
+                for turn, shift in enumerate(mp_shifts):
+                    act_chunks[turn + 1] += [lax.ppermute(piece, "mp", shift) for piece in acts]
         if step == 2:
-            down, up, meta = lax.optimization_barrier((down, up, meta))
+            down, up, acts, meta = lax.optimization_barrier((down, up, acts, meta))
         else:
-            down, up = lax.optimization_barrier((down, up))
-        grad_chunks += [down[0], up[0]]
-        act_chunks[0] += [down[1], up[1]]
-        for turn, shift in enumerate(mp_shifts):
-            act_chunks[turn + 1] += [lax.ppermute(piece[1], "mp", shift) for piece in (down, up)]
+            down, up, acts = lax.optimization_barrier((down, up, acts))
+        grad_chunks += [down, up]
     chunks = (grad_chunks, act_chunks)
 
     spots = meta[3]
@@ -410,32 +424,30 @@
         pairs = [(i, i ^ bit) for i in range(lax.axis_size(axis))]
         return value + lax.ppermute(value, axis, pairs)
 
-    bits = [1 << i for i in range((owners - 1).bit_length())]
-    core_bits = [1 << i for i in range((halves - 1).bit_length())]
     half_sq = piece_sq
+    sums = sum_steps(owners)
+    if 0 in sums:
+        half_sq = exchange(half_sq, "dp", sums[0])
+        upper, lower, half_sq = lax.optimization_barrier((upper, lower, half_sq))
+        downs, ups = [upper], [lower]
     for step in range(1, owners):
         after = (downs[-1], ups[-1]) if step > 1 else ()
         down = lax.ppermute(downs[-1], "dp", ahead)
         up = lax.ppermute(ups[-1], "dp", back)
-        kind = jobs[0][0] if jobs else None
         done = jobs.pop(0)[1](after) if jobs else half_sq
-        if kind == "left" and bits:
+        if step in sums:
             half_sq, done = lax.optimization_barrier((half_sq, done))
-            for bit in bits[:2]:
-                half_sq = exchange(half_sq, "dp", bit)
-            bits = bits[2:]
+            half_sq = exchange(half_sq, "dp", sums[step])
         if step < owners - 1:
             down, up, half_sq, _ = lax.optimization_barrier((down, up, half_sq, done))
         downs.append(down)
         ups.append(up)
     while jobs:
         jobs.pop(0)[1]((downs[-1], ups[-1]))
-    while bits:
-        half_sq = exchange(half_sq, "dp", bits.pop(0))
     for block in rest:
         half_sq = half_sq + rest[block][2]
-    while core_bits:
-        half_sq = exchange(half_sq, "mp", core_bits.pop(0))
+    for bit in [1 << i for i in range((halves - 1).bit_length())]:
+        half_sq = exchange(half_sq, "mp", bit)
     rescale = lax.rsqrt(half_sq / (row_blocks * BLK * half_width * halves) + 1.0)
 
     pieces = []
@@ -450,7 +462,8 @@
     cuts = [*range(0, early, limit), early, len(pieces)]
     for low, high in zip(cuts[:-1], cuts[1:]):
         group = pieces[low:high]
-        canvas = place_pieces(canvas, shape, spots, low, rescale, group)
+        late = late_count if low == early else 0
+        canvas = place_pieces(canvas, shape, spots, low, rescale, group, late)
     return canvas, roots[0][None]
 
 

time: 358 us -> 353 us (0.986)
  the two profiles are of different devices: /device:TPU:2 before, /device:TPU:0 now
where the time goes in v1:
time: 353 us; the launch traced here: 347 us
  Pallas kernels  167 us (47%)
  waiting for transfers between devices  95.5 us (27%)
  starting transfers between devices  61.6 us (17%)
  local copies, waits for them, and re-layouts  11.7 us (3%)
  between operations  5.86 us (2%)
  other arithmetic  4.63 us (1%)
    pallas_call x7, Pallas kernels, run_block(): pl.pallas_call(functools.partial(block_kernel, kind, owners, turns, len(a...  150 us
    ppermute x7, waiting for transfers between devices, shampoo_step(): lax.ppermute(acts[0], 'dp', ahead)  62.9 us
    pallas_call x2, Pallas kernels, place_pieces(): pl.pallas_call(functools.partial(place_kernel, first, count, late_count,...  17.6 us
    ppermute x7, starting transfers between devices, shampoo_step(): up = lax.ppermute(ups[-1], 'dp', back)  13 us
    ppermute x4, starting transfers between devices, exchange(): return value + lax.ppermute(value, axis, pairs)  12 us
    ppermute x7, waiting for transfers between devices, shampoo_step(): lax.ppermute(acts[1], 'dp', back)  11.2 us
    ppermute x7, starting transfers between devices, shampoo_step(): down = lax.ppermute(down, 'dp', ahead)  9.43 us
    ppermute x4, waiting for transfers between devices, exchange(): return value + lax.ppermute(value, axis, pairs)  8.72 us
  transfers between devices with their start and end apart: 61, of which 26 were waited for; matrix products, arithmetic and copies ran while one was open for 4% of the time, Pallas kernels for 38%

profile of v1, /device:TPU:0, one launch (start us, length us, event | category | flops | bytes accessed | tf_op | source)
XLA Modules:
  0.0 346.8 jit_solution(8734495278715034983)
XLA Ops:
  1.9 3.0 collective-permute-start.4
  5.1 1.4 fusion.9
  6.5 2.0 collective-permute-start.1
  16.9 2.0 collective-permute-start.5
  19.5 6.0 %collective-permute-done.5.refs_22_ = bf16[512,128]{1,0:T(8,128)(2,1)S(1)} collective-permute-done((bf16[512,128]{1,0:T(8,128)(2,1)S(1)}, bf16[512,128]{1,0:T(8,128)(2,1)S(1)}, u32[]{:S(2)}, u32[]{:S(2)}) %collective-permute-start.5) | collective-permute-done | bytes 131104 | tf_op jit(solution)/shard_map/ppermute | solution.py:391
  25.5 1.4 collective-permute-done.3.refs_21_
  27.4 1.6 collective-permute-start.7
  29.7 1.6 collective-permute-start.9
  34.1 10.4 %collective-permute-done.8.refs_23_ = bf16[512,128]{1,0:T(8,128)(2,1)S(1)} collective-permute-done((bf16[512,128]{1,0:T(8,128)(2,1)}, bf16[512,128]{1,0:T(8,128)(2,1)S(1)}, u32[]{:S(2)}, u32[]{:S(2)}) %collective-permute-start.8) | collective-permute-done | bytes 131104 | tf_op jit(solution)/shard_map/ppermute | solution.py:391
  45.0 1.6 collective-permute-start.10
  47.1 1.5 collective-permute-start.12
  49.1 12.7 %collective-permute-done.12.refs_25_ = bf16[512,128]{1,0:T(8,128)(2,1)S(1)} collective-permute-done((bf16[512,128]{1,0:T(8,128)(2,1)S(1)}, bf16[512,128]{1,0:T(8,128)(2,1)S(1)}, u32[]{:S(2)}, u32[]{:S(2)}) %collective-permute-start.12) | collective-permute-done | bytes 131104 | tf_op jit(solution)/shard_map/ppermute | solution.py:391
  63.2 1.8 collective-permute-start.14
  65.3 1.7 collective-permute-start.16
  67.3 12.7 %collective-permute-done.16.refs_27_ = bf16[512,128]{1,0:T(8,128)(2,1)S(1)} collective-permute-done((bf16[512,128]{1,0:T(8,128)(2,1)S(1)}, bf16[512,128]{1,0:T(8,128)(2,1)S(1)}, u32[]{:S(2)}, u32[]{:S(2)}) %collective-permute-start.16) | collective-permute-done | bytes 131104 | tf_op jit(solution)/shard_map/ppermute | solution.py:391
  80.0 1.5 collective-permute-done.17.refs_28_
  81.5 2.0 collective-permute-start.18
  83.6 1.9 collective-permute-start.20
  85.6 13.0 %collective-permute-done.20.refs_29_ = bf16[512,128]{1,0:T(8,128)(2,1)} collective-permute-done((bf16[512,128]{1,0:T(8,128)(2,1)S(1)}, bf16[512,128]{1,0:T(8,128)(2,1)}, u32[]{:S(2)}, u32[]{:S(2)}) %collective-permute-start.20) | collective-permute-done | bytes 131104 | tf_op jit(solution)/shard_map/ppermute | solution.py:391
  99.6 1.6 collective-permute-start.22
  101.7 1.6 collective-permute-start.24
  103.7 12.6 %collective-permute-done.24.refs_31_ = bf16[512,128]{1,0:T(8,128)(2,1)} collective-permute-done((bf16[512,128]{1,0:T(8,128)(2,1)}, bf16[512,128]{1,0:T(8,128)(2,1)}, u32[]{:S(2)}, u32[]{:S(2)}) %collective-permute-start.24) | collective-permute-done | bytes 131104 | tf_op jit(solution)/shard_map/ppermute | solution.py:391
  117.3 1.8 collective-permute-start.26
  125.7 2.2 collective-permute-done.26.refs_16_
  127.9 1.8 collective-permute-done.27.refs_17_
  130.7 1.7 collective-permute-done.42.refs_47_
  132.5 31.1 %shard_map.113 = (bf16[512,1024]{1,0:T(8,128)(2,1)}, bf16[512,1024]{1,0:T(8,128)(2,1)}, f32[1,1]{1,0:T(1,128)}) custom-call(s32[20]{0:T(128)} %reshape.422.refs_0_, f32[10]{0:T(128)} %reshape.423.refs_1_, s32[16]{0:T(128)} %pad_add_fusion.6.refs_2_, bf16[128,5120]{1,0:T(8,128)(2,1)} %refs_3_.13, bf16[64,5120]{1,0:T(8,128)(2,1)} %copy-done.14, ...), custom_call_target="tpu_custom_call" | custom-call | flops 27917287424 | bytes 12582912 | tf_op jit(solution)/shard_map/pallas_call | solution.py:219
  164.1 1.4 collective-permute-start.43
  165.5 2.4 collective-permute-done.43
  168.5 2.4 collective-permute-start.45
  170.9 14.5 %shard_map.114.refs_48_ = bf16[1024,1024]{1,0:T(8,128)(2,1)} custom-call(s32[20]{0:T(128)} %reshape.422.refs_0_, f32[10]{0:T(128)} %reshape.423.refs_1_, s32[16]{0:T(128)} %pad_add_fusion.6.refs_2_, bf16[128,5120]{1,0:T(8,128)(2,1)} %refs_3_.13, bf16[64,5120]{1,0:T(8,128)(2,1)} %copy-done.14, bf16[64,5120]{1,0:T(8,128)(2,1)} %copy-done.13, ...), custom_call_target="tpu_custom_call" | custom-call | flops 12884901888 | bytes 12582912 | tf_op jit(solution)/shard_map/pallas_call | solution.py:219
  185.4 5.2 %collective-permute-start.46 = (f32[1,1]{1,0:T(1,128)}, f32[1,1]{1,0:T(1,128)}, u32[]{:S(2)}, u32[]{:S(2)}) collective-permute-start(f32[1,1]{1,0:T(1,128)} %add.168), channel_id=1, source_target_pairs={{0,4},{2,6},{4,0},{6,2},{8,12},{10,14},{12,8},{14,10},{1,5},{3,7},... | collective-permute-start | bytes 20 | tf_op jit(solution)/shard_map/ppermute | solution.py:425
  190.5 2.7 collective-permute-done.46
  195.9 20.1 %shard_map.115 = (bf16[512,1024]{1,0:T(8,128)(2,1)}, bf16[512,1024]{1,0:T(8,128)(2,1)}, f32[1,1]{1,0:T(1,128)}) custom-call(s32[20]{0:T(128)} %reshape.422.refs_0_, f32[10]{0:T(128)} %reshape.423.refs_1_, s32[16]{0:T(128)} %pad_add_fusion.6.refs_2_, bf16[128,5120]{1,0:T(8,128)(2,1)} %refs_3_.13, bf16[64,5120]{1,0:T(8,128)(2,1)} %copy-done.14, ...), custom_call_target="tpu_custom_call" | custom-call | flops 17179869184 | bytes 12582912 | tf_op jit(solution)/shard_map/pallas_call | solution.py:219
  216.8 1.6 collective-permute-done.48.refs_49_.refs_11_
  218.4 2.0 collective-permute-start.49
  220.4 14.7 %shard_map.116.refs_48_ = bf16[1024,1024]{1,0:T(8,128)(2,1)} custom-call(s32[20]{0:T(128)} %reshape.422.refs_0_, f32[10]{0:T(128)} %reshape.423.refs_1_, s32[16]{0:T(128)} %pad_add_fusion.6.refs_2_, bf16[128,5120]{1,0:T(8,128)(2,1)} %refs_3_.13, bf16[64,5120]{1,0:T(8,128)(2,1)} %copy-done.14, bf16[64,5120]{1,0:T(8,128)(2,1)} %copy-done.13, ...), custom_call_target="tpu_custom_call" | custom-call | flops 12884901888 | bytes 12582912 | tf_op jit(solution)/shard_map/pallas_call | solution.py:219
  235.1 4.5 %collective-permute-start.51 = (f32[1,1]{1,0:T(1,128)}, f32[1,1]{1,0:T(1,128)}, u32[]{:S(2)}, u32[]{:S(2)}) collective-permute-start(f32[1,1]{1,0:T(1,128)} %add.169), channel_id=1, source_target_pairs={{0,8},{2,10},{4,12},{6,14},{8,0},{10,2},{12,4},{14,6},{1,9},{3,11}... | collective-permute-start | bytes 20 | tf_op jit(solution)/shard_map/ppermute | solution.py:425
  239.6 3.3 collective-permute-done.51
  243.6 2.0 collective-permute-start.53
  245.7 20.3 %shard_map.117 = (bf16[512,1024]{1,0:T(8,128)(2,1)}, bf16[512,1024]{1,0:T(8,128)(2,1)}, f32[1,1]{1,0:T(1,128)}) custom-call(s32[20]{0:T(128)} %reshape.422.refs_0_, f32[10]{0:T(128)} %reshape.423.refs_1_, s32[16]{0:T(128)} %pad_add_fusion.6.refs_2_, bf16[128,5120]{1,0:T(8,128)(2,1)} %refs_3_.13, bf16[64,5120]{1,0:T(8,128)(2,1)} %copy-done.14, ...), custom_call_target="tpu_custom_call" | custom-call | flops 17179869184 | bytes 12582912 | tf_op jit(solution)/shard_map/pallas_call | solution.py:219
  266.1 2.1 collective-permute-start.55
  268.3 23.0 %shard_map.118.refs_48_ = bf16[2,2,1024,1024]{3,2,1,0:T(8,128)(2,1)} custom-call(s32[20]{0:T(128)} %reshape.422.refs_0_, f32[10]{0:T(128)} %reshape.423.refs_1_, s32[16]{0:T(128)} %pad_add_fusion.6.refs_2_, bf16[128,5120]{1,0:T(8,128)(2,1)} %refs_3_.13, bf16[64,5120]{1,0:T(8,128)(2,1)} %copy-done.14, bf16[64,5120]{1,0:T(8,128)(2,1)} %copy-done.13, ...), custom_call_target="tpu_custom_call" | custom-call | flops 23622320128 | bytes 12582912 | tf_op jit(solution)/shard_map/pallas_call | solution.py:219
  291.5 3.5 %collective-permute-start.57 = (bf16[512,1024]{1,0:T(8,128)(2,1)S(1)}, bf16[512,1024]{1,0:T(8,128)(2,1)}, u32[]{:S(2)}, u32[]{:S(2)}) collective-permute-start(bf16[512,1024]{1,0:T(8,128)(2,1)S(1)} %collective-permute-done.55.refs_50_.refs_17_), channel_id=1, source_target_pairs={{4,0},{8,4},{12,8},{14,12},{10,14},{6,10},{2,6},{0,2},{5,1},{9,5},... | collective-permute-start | bytes 3145736 | tf_op jit(solution)/shard_map/ppermute | solution.py:436
  294.9 26.2 %shard_map.119 = bf16[2,2,1024,1024]{3,2,1,0:T(8,128)(2,1)} custom-call(s32[20]{0:T(128)} %reshape.422.refs_0_, f32[10]{0:T(128)} %reshape.423.refs_1_, s32[16]{0:T(128)} %pad_add_fusion.6.refs_2_, bf16[128,5120]{1,0:T(8,128)(2,1)} %refs_3_.13, bf16[64,5120]{1,0:T(8,128)(2,1)} %copy-done.14, ...), custom_call_target="tpu_custom_call", output_to_operand_aliasing={{}: (48, {})} | custom-call | flops 23622320128 | bytes 12582912 | tf_op jit(solution)/shard_map/pallas_call | solution.py:219
  321.2 2.2 collective-permute-start.60
  326.8 14.5 %place.2.refs_4_ = bf16[2048,5120]{1,0:T(8,128)(2,1)} custom-call(s32[40]{0:T(128)} %reshape.424.refs_0_, f32[1,1]{1,0:T(1,128)S(6)} %rsqrt.3.refs_1_, bf16[512,1024]{1,0:T(8,128)(2,1)} %get-tuple-element.100.refs_2_, bf16[512,1024]{1,0:T(8,128)(2,1)} %get-tuple-element.120.refs_3_, bf16[512,1024]{1,0:T(8,128)(2,1)} %get-tuple-element.108.refs_4_, ...), custom_call_target="tpu_custom_call" | custom-call | flops 1887436800 | bytes 37748736 | tf_op jit(solution)/shard_map/place/pallas_call | solution.py:284
  343.3 3.1 place.3
  (213 shorter events, 35.0 us)
Async XLA Ops:
  1.9 14.9 %collective-permute-start.4 = (bf16[512,128]{1,0:T(8,128)(2,1)S(1)}, bf16[512,128]{1,0:T(8,128)(2,1)S(1)}, u32[]{:S(2)}, u32[]{:S(2)}) collective-permute-start(bf16[512,128]{1,0:T(8,128)(2,1)S(1)} %get-tuple-element.128), channel_id=1, source_target_pairs={{4,0},{8,4},{12,8},{14,12},{10,14},{6,10},{2,6},{0,2},{5,1},{9,5},... | collective-permute-start | bytes 393224 | tf_op jit(solution)/shard_map/ppermute | solution.py:391
  5.0 13.9 %collective-permute-start.2 = (bf16[512,128]{1,0:T(8,128)(2,1)S(1)}, bf16[512,128]{1,0:T(8,128)(2,1)S(1)}, u32[]{:S(2)}, u32[]{:S(2)}) collective-permute-start(bf16[512,128]{1,0:T(8,128)(2,1)S(1)} %get-tuple-element.129), channel_id=1, source_target_pairs={{0,4},{4,8},{8,12},{12,14},{14,10},{10,6},{6,2},{2,0},{1,5},{5,9},... | collective-permute-start | bytes 393224 | tf_op jit(solution)/shard_map/ppermute | solution.py:391
  6.5 20.5 %collective-permute-start.1 = (bf16[64,5120]{1,0:T(8,128)(2,1)S(1)}, bf16[64,5120]{1,0:T(8,128)(2,1)S(1)}, u32[]{:S(2)}, u32[]{:S(2)}) collective-permute-start(bf16[64,5120]{1,0:T(8,128)(2,1)S(1)} %get-tuple-element.126), channel_id=1, source_target_pairs={{4,0},{8,4},{12,8},{14,12},{10,14},{6,10},{2,6},{0,2},{5,1},{9,5},... | collective-permute-start | bytes 1966088 | tf_op jit(solution)/shard_map/ppermute | solution.py:388
  8.4 18.6 %collective-permute-start = (bf16[64,5120]{1,0:T(8,128)(2,1)S(1)}, bf16[64,5120]{1,0:T(8,128)(2,1)S(1)}, u32[]{:S(2)}, u32[]{:S(2)}) collective-permute-start(bf16[64,5120]{1,0:T(8,128)(2,1)S(1)} %get-tuple-element.127), channel_id=1, source_target_pairs={{0,4},{4,8},{8,12},{12,14},{14,10},{10,6},{6,2},{2,0},{1,5},{5,9},... | collective-permute-start | bytes 1966088 | tf_op jit(solution)/shard_map/ppermute | solution.py:387
  16.9 8.7 %collective-permute-start.5 = (bf16[512,128]{1,0:T(8,128)(2,1)S(1)}, bf16[512,128]{1,0:T(8,128)(2,1)S(1)}, u32[]{:S(2)}, u32[]{:S(2)}) collective-permute-start(bf16[512,128]{1,0:T(8,128)(2,1)S(1)} %collective-permute-done.4.refs_20_), channel_id=1, source_target_pairs={{4,0},{8,4},{12,8},{14,12},{10,14},{6,10},{2,6},{0,2},{5,1},{9,5},... | collective-permute-start | bytes 393224 | tf_op jit(solution)/shard_map/ppermute | solution.py:391
  18.8 8.1 %collective-permute-start.3 = (bf16[512,128]{1,0:T(8,128)(2,1)S(1)}, bf16[512,128]{1,0:T(8,128)(2,1)}, u32[]{:S(2)}, u32[]{:S(2)}) collective-permute-start(bf16[512,128]{1,0:T(8,128)(2,1)S(1)} %collective-permute-done.2.refs_19_), channel_id=1, source_target_pairs={{0,4},{4,8},{8,12},{12,14},{14,10},{10,6},{6,2},{2,0},{1,5},{5,9},... | collective-permute-start | bytes 393224 | tf_op jit(solution)/shard_map/ppermute | solution.py:391
  27.0 18.0 %collective-permute-start.6 = (bf16[64,5120]{1,0:T(8,128)(2,1)S(1)}, bf16[64,5120]{1,0:T(8,128)(2,1)S(1)}, u32[]{:S(2)}, u32[]{:S(2)}) collective-permute-start(bf16[64,5120]{1,0:T(8,128)(2,1)S(1)} %collective-permute-done.refs_4_), channel_id=1, source_target_pairs={{0,4},{4,8},{8,12},{12,14},{14,10},{10,6},{6,2},{2,0},{1,5},{5,9},... | collective-permute-start | bytes 1966088 | tf_op jit(solution)/shard_map/ppermute | solution.py:387
  27.4 17.6 %collective-permute-start.7 = (bf16[64,5120]{1,0:T(8,128)(2,1)S(1)}, bf16[64,5120]{1,0:T(8,128)(2,1)}, u32[]{:S(2)}, u32[]{:S(2)}) collective-permute-start(bf16[64,5120]{1,0:T(8,128)(2,1)S(1)} %collective-permute-done.1.refs_5_), channel_id=1, source_target_pairs={{4,0},{8,4},{12,8},{14,12},{10,14},{6,10},{2,6},{0,2},{5,1},{9,5},... | collective-permute-start | bytes 1966088 | tf_op jit(solution)/shard_map/ppermute | solution.py:388
  29.2 15.3 %collective-permute-start.8 = (bf16[512,128]{1,0:T(8,128)(2,1)}, bf16[512,128]{1,0:T(8,128)(2,1)S(1)}, u32[]{:S(2)}, u32[]{:S(2)}) collective-permute-start(bf16[512,128]{1,0:T(8,128)(2,1)} %collective-permute-done.3.refs_21_), channel_id=1, source_target_pairs={{0,4},{4,8},{8,12},{12,14},{14,10},{10,6},{6,2},{2,0},{1,5},{5,9},... | collective-permute-start | bytes 393224 | tf_op jit(solution)/shard_map/ppermute | solution.py:391
  29.7 15.3 %collective-permute-start.9 = (bf16[512,128]{1,0:T(8,128)(2,1)S(1)}, bf16[512,128]{1,0:T(8,128)(2,1)}, u32[]{:S(2)}, u32[]{:S(2)}) collective-permute-start(bf16[512,128]{1,0:T(8,128)(2,1)S(1)} %collective-permute-done.5.refs_22_), channel_id=1, source_target_pairs={{4,0},{8,4},{12,8},{14,12},{10,14},{6,10},{2,6},{0,2},{5,1},{9,5},... | collective-permute-start | bytes 393224 | tf_op jit(solution)/shard_map/ppermute | solution.py:391
  45.0 18.1 %collective-permute-start.10 = (bf16[64,5120]{1,0:T(8,128)(2,1)S(1)}, bf16[64,5120]{1,0:T(8,128)(2,1)S(1)}, u32[]{:S(2)}, u32[]{:S(2)}) collective-permute-start(bf16[64,5120]{1,0:T(8,128)(2,1)S(1)} %collective-permute-done.6.refs_6_), channel_id=1, source_target_pairs={{0,4},{4,8},{8,12},{12,14},{14,10},{10,6},{6,2},{2,0},{1,5},{5,9},... | collective-permute-start | bytes 1966088 | tf_op jit(solution)/shard_map/ppermute | solution.py:387
  46.6 16.6 %collective-permute-start.11 = (bf16[64,5120]{1,0:T(8,128)(2,1)}, bf16[64,5120]{1,0:T(8,128)(2,1)S(1)}, u32[]{:S(2)}, u32[]{:S(2)}) collective-permute-start(bf16[64,5120]{1,0:T(8,128)(2,1)} %collective-permute-done.7.refs_7_), channel_id=1, source_target_pairs={{4,0},{8,4},{12,8},{14,12},{10,14},{6,10},{2,6},{0,2},{5,1},{9,5},... | collective-permute-start | bytes 1966088 | tf_op jit(solution)/shard_map/ppermute | solution.py:388
  47.1 14.7 %collective-permute-start.12 = (bf16[512,128]{1,0:T(8,128)(2,1)S(1)}, bf16[512,128]{1,0:T(8,128)(2,1)S(1)}, u32[]{:S(2)}, u32[]{:S(2)}) collective-permute-start(bf16[512,128]{1,0:T(8,128)(2,1)S(1)} %collective-permute-done.8.refs_23_), channel_id=1, source_target_pairs={{0,4},{4,8},{8,12},{12,14},{14,10},{10,6},{6,2},{2,0},{1,5},{5,9},... | collective-permute-start | bytes 393224 | tf_op jit(solution)/shard_map/ppermute | solution.py:391
  48.6 14.5 %collective-permute-start.13 = (bf16[512,128]{1,0:T(8,128)(2,1)}, bf16[512,128]{1,0:T(8,128)(2,1)S(1)}, u32[]{:S(2)}, u32[]{:S(2)}) collective-permute-start(bf16[512,128]{1,0:T(8,128)(2,1)} %collective-permute-done.9.refs_24_), channel_id=1, source_target_pairs={{4,0},{8,4},{12,8},{14,12},{10,14},{6,10},{2,6},{0,2},{5,1},{9,5},... | collective-permute-start | bytes 393224 | tf_op jit(solution)/shard_map/ppermute | solution.py:391
  63.2 18.3 %collective-permute-start.14 = (bf16[64,5120]{1,0:T(8,128)(2,1)S(1)}, bf16[64,5120]{1,0:T(8,128)(2,1)S(1)}, u32[]{:S(2)}, u32[]{:S(2)}) collective-permute-start(bf16[64,5120]{1,0:T(8,128)(2,1)S(1)} %collective-permute-done.10.refs_8_), channel_id=1, source_target_pairs={{0,4},{4,8},{8,12},{12,14},{14,10},{10,6},{6,2},{2,0},{1,5},{5,9},... | collective-permute-start | bytes 1966088 | tf_op jit(solution)/shard_map/ppermute | solution.py:387
  65.0 16.5 %collective-permute-start.15 = (bf16[64,5120]{1,0:T(8,128)(2,1)S(1)}, bf16[64,5120]{1,0:T(8,128)(2,1)S(1)}, u32[]{:S(2)}, u32[]{:S(2)}) collective-permute-start(bf16[64,5120]{1,0:T(8,128)(2,1)S(1)} %collective-permute-done.11.refs_9_), channel_id=1, source_target_pairs={{4,0},{8,4},{12,8},{14,12},{10,14},{6,10},{2,6},{0,2},{5,1},{9,5},... | collective-permute-start | bytes 1966088 | tf_op jit(solution)/shard_map/ppermute | solution.py:388
  65.3 14.7 %collective-permute-start.16 = (bf16[512,128]{1,0:T(8,128)(2,1)S(1)}, bf16[512,128]{1,0:T(8,128)(2,1)S(1)}, u32[]{:S(2)}, u32[]{:S(2)}) collective-permute-start(bf16[512,128]{1,0:T(8,128)(2,1)S(1)} %collective-permute-done.12.refs_25_), channel_id=1, source_target_pairs={{0,4},{4,8},{8,12},{12,14},{14,10},{10,6},{6,2},{2,0},{1,5},{5,9},... | collective-permute-start | bytes 393224 | tf_op jit(solution)/shard_map/ppermute | solution.py:391
  67.0 14.5 %collective-permute-start.17 = (bf16[512,128]{1,0:T(8,128)(2,1)S(1)}, bf16[512,128]{1,0:T(8,128)(2,1)}, u32[]{:S(2)}, u32[]{:S(2)}) collective-permute-start(bf16[512,128]{1,0:T(8,128)(2,1)S(1)} %collective-permute-done.13.refs_26_), channel_id=1, source_target_pairs={{4,0},{8,4},{12,8},{14,12},{10,14},{6,10},{2,6},{0,2},{5,1},{9,5},... | collective-permute-start | bytes 393224 | tf_op jit(solution)/shard_map/ppermute | solution.py:391
  81.5 18.1 %collective-permute-start.18 = (bf16[64,5120]{1,0:T(8,128)(2,1)S(1)}, bf16[64,5120]{1,0:T(8,128)(2,1)S(1)}, u32[]{:S(2)}, u32[]{:S(2)}) collective-permute-start(bf16[64,5120]{1,0:T(8,128)(2,1)S(1)} %collective-permute-done.14.refs_10_), channel_id=1, source_target_pairs={{0,4},{4,8},{8,12},{12,14},{14,10},{10,6},{6,2},{2,0},{1,5},{5,9},... | collective-permute-start | bytes 1966088 | tf_op jit(solution)/shard_map/ppermute | solution.py:387
  83.5 16.1 %collective-permute-start.19 = (bf16[64,5120]{1,0:T(8,128)(2,1)S(1)}, bf16[64,5120]{1,0:T(8,128)(2,1)S(1)}, u32[]{:S(2)}, u32[]{:S(2)}) collective-permute-start(bf16[64,5120]{1,0:T(8,128)(2,1)S(1)} %collective-permute-done.15.refs_11_), channel_id=1, source_target_pairs={{4,0},{8,4},{12,8},{14,12},{10,14},{6,10},{2,6},{0,2},{5,1},{9,5},... | collective-permute-start | bytes 1966088 | tf_op jit(solution)/shard_map/ppermute | solution.py:388
  83.6 15.0 %collective-permute-start.20 = (bf16[512,128]{1,0:T(8,128)(2,1)S(1)}, bf16[512,128]{1,0:T(8,128)(2,1)}, u32[]{:S(2)}, u32[]{:S(2)}) collective-permute-start(bf16[512,128]{1,0:T(8,128)(2,1)S(1)} %collective-permute-done.16.refs_27_), channel_id=1, source_target_pairs={{0,4},{4,8},{8,12},{12,14},{14,10},{10,6},{6,2},{2,0},{1,5},{5,9},... | collective-permute-start | bytes 393224 | tf_op jit(solution)/shard_map/ppermute | solution.py:391
  85.5 14.0 %collective-permute-start.21 = (bf16[512,128]{1,0:T(8,128)(2,1)}, bf16[512,128]{1,0:T(8,128)(2,1)}, u32[]{:S(2)}, u32[]{:S(2)}) collective-permute-start(bf16[512,128]{1,0:T(8,128)(2,1)} %collective-permute-done.17.refs_28_), channel_id=1, source_target_pairs={{4,0},{8,4},{12,8},{14,12},{10,14},{6,10},{2,6},{0,2},{5,1},{9,5},... | collective-permute-start | bytes 393224 | tf_op jit(solution)/shard_map/ppermute | solution.py:391
  99.6 17.7 %collective-permute-start.22 = (bf16[64,5120]{1,0:T(8,128)(2,1)S(1)}, bf16[64,5120]{1,0:T(8,128)(2,1)S(1)}, u32[]{:S(2)}, u32[]{:S(2)}) collective-permute-start(bf16[64,5120]{1,0:T(8,128)(2,1)S(1)} %collective-permute-done.18.refs_12_), channel_id=1, source_target_pairs={{0,4},{4,8},{8,12},{12,14},{14,10},{10,6},{6,2},{2,0},{1,5},{5,9},... | collective-permute-start | bytes 1966088 | tf_op jit(solution)/shard_map/ppermute | solution.py:387
  101.2 16.1 %collective-permute-start.23 = (bf16[64,5120]{1,0:T(8,128)(2,1)S(1)}, bf16[64,5120]{1,0:T(8,128)(2,1)S(1)}, u32[]{:S(2)}, u32[]{:S(2)}) collective-permute-start(bf16[64,5120]{1,0:T(8,128)(2,1)S(1)} %collective-permute-done.19.refs_13_), channel_id=1, source_target_pairs={{4,0},{8,4},{12,8},{14,12},{10,14},{6,10},{2,6},{0,2},{5,1},{9,5},... | collective-permute-start | bytes 1966088 | tf_op jit(solution)/shard_map/ppermute | solution.py:388
  101.7 14.7 %collective-permute-start.24 = (bf16[512,128]{1,0:T(8,128)(2,1)}, bf16[512,128]{1,0:T(8,128)(2,1)}, u32[]{:S(2)}, u32[]{:S(2)}) collective-permute-start(bf16[512,128]{1,0:T(8,128)(2,1)} %collective-permute-done.20.refs_29_), channel_id=1, source_target_pairs={{0,4},{4,8},{8,12},{12,14},{14,10},{10,6},{6,2},{2,0},{1,5},{5,9},... | collective-permute-start | bytes 393224 | tf_op jit(solution)/shard_map/ppermute | solution.py:391
  103.2 14.0 %collective-permute-start.25 = (bf16[512,128]{1,0:T(8,128)(2,1)}, bf16[512,128]{1,0:T(8,128)(2,1)}, u32[]{:S(2)}, u32[]{:S(2)}) collective-permute-start(bf16[512,128]{1,0:T(8,128)(2,1)} %collective-permute-done.21.refs_30_), channel_id=1, source_target_pairs={{4,0},{8,4},{12,8},{14,12},{10,14},{6,10},{2,6},{0,2},{5,1},{9,5},... | collective-permute-start | bytes 393224 | tf_op jit(solution)/shard_map/ppermute | solution.py:391
  117.3 10.6 %collective-permute-start.26 = (bf16[64,5120]{1,0:T(8,128)(2,1)S(1)}, bf16[64,5120]{1,0:T(8,128)(2,1)S(1)}, u32[]{:S(2)}, u32[]{:S(2)}) collective-permute-start(bf16[64,5120]{1,0:T(8,128)(2,1)S(1)} %collective-permute-done.22.refs_14_), channel_id=1, source_target_pairs={{0,4},{4,8},{8,12},{12,14},{14,10},{10,6},{6,2},{2,0},{1,5},{5,9},... | collective-permute-start | bytes 1966088 | tf_op jit(solution)/shard_map/ppermute | solution.py:387
  119.1 10.6 %collective-permute-start.27 = (bf16[64,5120]{1,0:T(8,128)(2,1)S(1)}, bf16[64,5120]{1,0:T(8,128)(2,1)S(1)}, u32[]{:S(2)}, u32[]{:S(2)}) collective-permute-start(bf16[64,5120]{1,0:T(8,128)(2,1)S(1)} %collective-permute-done.23.refs_15_), channel_id=1, source_target_pairs={{4,0},{8,4},{12,8},{14,12},{10,14},{6,10},{2,6},{0,2},{5,1},{9,5},... | collective-permute-start | bytes 1966088 | tf_op jit(solution)/shard_map/ppermute | solution.py:388
  124.4 6.3 %collective-permute-start.38 = (bf16[512,128]{1,0:T(8,128)(2,1)}, bf16[512,128]{1,0:T(8,128)(2,1)}, u32[]{:S(2)}, u32[]{:S(2)}) collective-permute-start(bf16[512,128]{1,0:T(8,128)(2,1)} %collective-permute-done.17.refs_28_), channel_id=1, source_target_pairs={{0,1},{1,0},{2,3},{3,2},{4,5},{5,4},{6,7},{7,6},{8,9},{9,8},{10,11... | collective-permute-start | bytes 393224 | tf_op jit(solution)/shard_map/ppermute | solution.py:394
  124.7 6.0 %collective-permute-start.39 = (bf16[512,128]{1,0:T(8,128)(2,1)}, bf16[512,128]{1,0:T(8,128)(2,1)}, u32[]{:S(2)}, u32[]{:S(2)}) collective-permute-start(bf16[512,128]{1,0:T(8,128)(2,1)} %collective-permute-done.20.refs_29_), channel_id=1, source_target_pairs={{0,1},{1,0},{2,3},{3,2},{4,5},{5,4},{6,7},{7,6},{8,9},{9,8},{10,11... | collective-permute-start | bytes 393224 | tf_op jit(solution)/shard_map/ppermute | solution.py:394
  125.6 5.1 %collective-permute-start.40 = (bf16[512,128]{1,0:T(8,128)(2,1)}, bf16[512,128]{1,0:T(8,128)(2,1)}, u32[]{:S(2)}, u32[]{:S(2)}) collective-permute-start(bf16[512,128]{1,0:T(8,128)(2,1)} %collective-permute-done.21.refs_30_), channel_id=1, source_target_pairs={{0,1},{1,0},{2,3},{3,2},{4,5},{5,4},{6,7},{7,6},{8,9},{9,8},{10,11... | collective-permute-start | bytes 393224 | tf_op jit(solution)/shard_map/ppermute | solution.py:394
  164.1 3.7 %collective-permute-start.43 = (f32[1,1]{1,0:T(1,128)}, f32[1,1]{1,0:T(1,128)}, u32[]{:S(2)}, u32[]{:S(2)}) collective-permute-start(f32[1,1]{1,0:T(1,128)} %select_n.161), channel_id=1, source_target_pairs={{0,2},{2,0},{4,6},{6,4},{8,10},{10,8},{12,14},{14,12},{1,3},{3,1},... | collective-permute-start | bytes 20 | tf_op jit(solution)/shard_map/ppermute | solution.py:425
  168.4 25.3 %collective-permute-start.44 = (bf16[512,1024]{1,0:T(8,128)(2,1)}, bf16[512,1024]{1,0:T(8,128)(2,1)S(1)}, u32[]{:S(2)}, u32[]{:S(2)}) collective-permute-start(bf16[512,1024]{1,0:T(8,128)(2,1)} %get-tuple-element.93.refs_6_), channel_id=1, source_target_pairs={{0,4},{4,8},{8,12},{12,14},{14,10},{10,6},{6,2},{2,0},{1,5},{5,9},... | collective-permute-start | bytes 3145736 | tf_op jit(solution)/shard_map/ppermute | solution.py:435
  168.5 25.3 %collective-permute-start.45 = (bf16[512,1024]{1,0:T(8,128)(2,1)}, bf16[512,1024]{1,0:T(8,128)(2,1)S(1)}, u32[]{:S(2)}, u32[]{:S(2)}) collective-permute-start(bf16[512,1024]{1,0:T(8,128)(2,1)} %get-tuple-element.94.refs_7_), channel_id=1, source_target_pairs={{4,0},{8,4},{12,8},{14,12},{10,14},{6,10},{2,6},{0,2},{5,1},{9,5},... | collective-permute-start | bytes 3145736 | tf_op jit(solution)/shard_map/ppermute | solution.py:436
  185.4 7.8 %collective-permute-start.46 = (f32[1,1]{1,0:T(1,128)}, f32[1,1]{1,0:T(1,128)}, u32[]{:S(2)}, u32[]{:S(2)}) collective-permute-start(f32[1,1]{1,0:T(1,128)} %add.168), channel_id=1, source_target_pairs={{0,4},{2,6},{4,0},{6,2},{8,12},{10,14},{12,8},{14,10},{1,5},{3,7},... | collective-permute-start | bytes 20 | tf_op jit(solution)/shard_map/ppermute | solution.py:425
  193.8 23.0 %collective-permute-start.47 = (bf16[512,1024]{1,0:T(8,128)(2,1)S(1)}, bf16[512,1024]{1,0:T(8,128)(2,1)S(1)}, u32[]{:S(2)}, u32[]{:S(2)}) collective-permute-start(bf16[512,1024]{1,0:T(8,128)(2,1)S(1)} %collective-permute-done.44.refs_49_.refs_8_), channel_id=1, source_target_pairs={{0,4},{4,8},{8,12},{12,14},{14,10},{10,6},{6,2},{2,0},{1,5},{5,9},... | collective-permute-start | bytes 3145736 | tf_op jit(solution)/shard_map/ppermute | solution.py:435
  195.1 23.3 %collective-permute-start.48 = (bf16[512,1024]{1,0:T(8,128)(2,1)S(1)}, bf16[512,1024]{1,0:T(8,128)(2,1)}, u32[]{:S(2)}, u32[]{:S(2)}) collective-permute-start(bf16[512,1024]{1,0:T(8,128)(2,1)S(1)} %collective-permute-done.45.refs_50_.refs_9_), channel_id=1, source_target_pairs={{4,0},{8,4},{12,8},{14,12},{10,14},{6,10},{2,6},{0,2},{5,1},{9,5},... | collective-permute-start | bytes 3145736 | tf_op jit(solution)/shard_map/ppermute | solution.py:436
  218.4 25.2 %collective-permute-start.49 = (bf16[512,1024]{1,0:T(8,128)(2,1)S(1)}, bf16[512,1024]{1,0:T(8,128)(2,1)S(1)}, u32[]{:S(2)}, u32[]{:S(2)}) collective-permute-start(bf16[512,1024]{1,0:T(8,128)(2,1)S(1)} %collective-permute-done.47.refs_48_.refs_10_), channel_id=1, source_target_pairs={{0,4},{4,8},{8,12},{12,14},{14,10},{10,6},{6,2},{2,0},{1,5},{5,9},... | collective-permute-start | bytes 3145736 | tf_op jit(solution)/shard_map/ppermute | solution.py:435
  220.4 23.2 %collective-permute-start.50 = (bf16[512,1024]{1,0:T(8,128)(2,1)}, bf16[512,1024]{1,0:T(8,128)(2,1)S(1)}, u32[]{:S(2)}, u32[]{:S(2)}) collective-permute-start(bf16[512,1024]{1,0:T(8,128)(2,1)} %collective-permute-done.48.refs_49_.refs_11_), channel_id=1, source_target_pairs={{4,0},{8,4},{12,8},{14,12},{10,14},{6,10},{2,6},{0,2},{5,1},{9,5},... | collective-permute-start | bytes 3145736 | tf_op jit(solution)/shard_map/ppermute | solution.py:436
  235.1 7.8 %collective-permute-start.51 = (f32[1,1]{1,0:T(1,128)}, f32[1,1]{1,0:T(1,128)}, u32[]{:S(2)}, u32[]{:S(2)}) collective-permute-start(f32[1,1]{1,0:T(1,128)} %add.169), channel_id=1, source_target_pairs={{0,8},{2,10},{4,12},{6,14},{8,0},{10,2},{12,4},{14,6},{1,9},{3,11}... | collective-permute-start | bytes 20 | tf_op jit(solution)/shard_map/ppermute | solution.py:425
  243.6 22.4 %collective-permute-start.52 = (bf16[512,1024]{1,0:T(8,128)(2,1)S(1)}, bf16[512,1024]{1,0:T(8,128)(2,1)S(1)}, u32[]{:S(2)}, u32[]{:S(2)}) collective-permute-start(bf16[512,1024]{1,0:T(8,128)(2,1)S(1)} %collective-permute-done.49.refs_49_.refs_12_), channel_id=1, source_target_pairs={{0,4},{4,8},{8,12},{12,14},{14,10},{10,6},{6,2},{2,0},{1,5},{5,9},... | collective-permute-start | bytes 3145736 | tf_op jit(solution)/shard_map/ppermute | solution.py:435
  243.6 22.4 %collective-permute-start.53 = (bf16[512,1024]{1,0:T(8,128)(2,1)S(1)}, bf16[512,1024]{1,0:T(8,128)(2,1)}, u32[]{:S(2)}, u32[]{:S(2)}) collective-permute-start(bf16[512,1024]{1,0:T(8,128)(2,1)S(1)} %collective-permute-done.50.refs_50_.refs_13_), channel_id=1, source_target_pairs={{4,0},{8,4},{12,8},{14,12},{10,14},{6,10},{2,6},{0,2},{5,1},{9,5},... | collective-permute-start | bytes 3145736 | tf_op jit(solution)/shard_map/ppermute | solution.py:436
  266.0 25.3 %collective-permute-start.54 = (bf16[512,1024]{1,0:T(8,128)(2,1)S(1)}, bf16[512,1024]{1,0:T(8,128)(2,1)S(1)}, u32[]{:S(2)}, u32[]{:S(2)}) collective-permute-start(bf16[512,1024]{1,0:T(8,128)(2,1)S(1)} %collective-permute-done.52.refs_48_.refs_14_), channel_id=1, source_target_pairs={{0,4},{4,8},{8,12},{12,14},{14,10},{10,6},{6,2},{2,0},{1,5},{5,9},... | collective-permute-start | bytes 3145736 | tf_op jit(solution)/shard_map/ppermute | solution.py:435
  266.1 25.2 %collective-permute-start.55 = (bf16[512,1024]{1,0:T(8,128)(2,1)}, bf16[512,1024]{1,0:T(8,128)(2,1)S(1)}, u32[]{:S(2)}, u32[]{:S(2)}) collective-permute-start(bf16[512,1024]{1,0:T(8,128)(2,1)} %collective-permute-done.53.refs_49_.refs_15_), channel_id=1, source_target_pairs={{4,0},{8,4},{12,8},{14,12},{10,14},{6,10},{2,6},{0,2},{5,1},{9,5},... | collective-permute-start | bytes 3145736 | tf_op jit(solution)/shard_map/ppermute | solution.py:436
  291.3 29.8 %collective-permute-start.56 = (bf16[512,1024]{1,0:T(8,128)(2,1)S(1)}, bf16[512,1024]{1,0:T(8,128)(2,1)S(1)}, u32[]{:S(2)}, u32[]{:S(2)}) collective-permute-start(bf16[512,1024]{1,0:T(8,128)(2,1)S(1)} %collective-permute-done.54.refs_49_.refs_16_), channel_id=1, source_target_pairs={{0,4},{4,8},{8,12},{12,14},{14,10},{10,6},{6,2},{2,0},{1,5},{5,9},... | collective-permute-start | bytes 3145736 | tf_op jit(solution)/shard_map/ppermute | solution.py:435
  291.5 29.7 %collective-permute-start.57 = (bf16[512,1024]{1,0:T(8,128)(2,1)S(1)}, bf16[512,1024]{1,0:T(8,128)(2,1)}, u32[]{:S(2)}, u32[]{:S(2)}) collective-permute-start(bf16[512,1024]{1,0:T(8,128)(2,1)S(1)} %collective-permute-done.55.refs_50_.refs_17_), channel_id=1, source_target_pairs={{4,0},{8,4},{12,8},{14,12},{10,14},{6,10},{2,6},{0,2},{5,1},{9,5},... | collective-permute-start | bytes 3145736 | tf_op jit(solution)/shard_map/ppermute | solution.py:436
  321.2 20.1 %collective-permute-start.59 = (bf16[512,1024]{1,0:T(8,128)(2,1)S(1)}, bf16[512,1024]{1,0:T(8,128)(2,1)S(1)}, u32[]{:S(2)}, u32[]{:S(2)}) collective-permute-start(bf16[512,1024]{1,0:T(8,128)(2,1)S(1)} %collective-permute-done.56.refs_18_), channel_id=1, source_target_pairs={{0,4},{4,8},{8,12},{12,14},{14,10},{10,6},{6,2},{2,0},{1,5},{5,9},... | collective-permute-start | bytes 3145736 | tf_op jit(solution)/shard_map/ppermute | solution.py:435
  321.2 22.1 %collective-permute-start.60 = (bf16[512,1024]{1,0:T(8,128)(2,1)}, bf16[512,1024]{1,0:T(8,128)(2,1)}, u32[]{:S(2)}, u32[]{:S(2)}) collective-permute-start(bf16[512,1024]{1,0:T(8,128)(2,1)} %collective-permute-done.57.refs_19_), channel_id=1, source_target_pairs={{4,0},{8,4},{12,8},{14,12},{10,14},{6,10},{2,6},{0,2},{5,1},{9,5},... | collective-permute-start | bytes 3145736 | tf_op jit(solution)/shard_map/ppermute | solution.py:436
  (56 other events, 1421.7 us)

commit v2 on v1

--- a/solution.py
+++ b/solution.py
@@ -111,8 +111,13 @@
         symmetric_product(raised.at[0], 0, rounded, (raised.at[1],))
 
     moved = wide_dot(raised[quartic], current[...], 1, 0)
-    eye = diagonal(moved.shape)
-    later[...] = ((jnp.where(eye, root_order + 1.0, 0.0) - moved) * inverse).astype(jnp.bfloat16)
+    later[...] = (moved * -inverse).astype(jnp.bfloat16)
+    for low in range(0, BLK, TILE):
+        near = slice(low, low + TILE)
+        tile = moved[near, near]
+        eye = diagonal(tile.shape)
+        tile = (jnp.where(eye, root_order + 1.0, 0.0) - tile) * inverse
+        later[near, near] = tile.astype(jnp.bfloat16)
     root[...] = wide_dot(factor[...], later[...], 1, 0).astype(jnp.bfloat16)
 
 
@@ -144,7 +149,9 @@
         ints, places, (owners, turns, tok, grad_refs, act_refs), acts_t, grads, sems
     )
     block_grad = wide_dot(acts_t[...], grads[...], 1, 0)
-    block_grad = jnp.where(ints[3] != 0, block_grad, 0.0).astype(jnp.bfloat16)
+    if kind == "roots":
+        block_grad = jnp.where(ints[3] != 0, block_grad, 0.0)
+    block_grad = block_grad.astype(jnp.bfloat16)
     gradient[0] = block_grad
     if kind != "left":
         gradient[1] = block_grad.T

time: 353 us -> 353 us (level)
  no operation moved by 1% of the time
where the time goes in v2:
time: 353 us; the launch traced here: 347 us
  Pallas kernels  167 us (47%)
  waiting for transfers between devices  95.6 us (27%)
  starting transfers between devices  61.7 us (17%)
  local copies, waits for them, and re-layouts  11.7 us (3%)
  between operations  5.86 us (2%)
  other arithmetic  4.63 us (1%)
    pallas_call x7, Pallas kernels, run_block(): pl.pallas_call(functools.partial(block_kernel, kind, owners, turns, len(a...  150 us
    ppermute x7, waiting for transfers between devices, shampoo_step(): lax.ppermute(acts[0], 'dp', ahead)  62.9 us
    pallas_call x2, Pallas kernels, place_pieces(): pl.pallas_call(functools.partial(place_kernel, first, count, late_count,...  17.6 us
    ppermute x7, starting transfers between devices, shampoo_step(): up = lax.ppermute(ups[-1], 'dp', back)  13 us
    ppermute x4, starting transfers between devices, exchange(): return value + lax.ppermute(value, axis, pairs)  12.1 us
    ppermute x7, waiting for transfers between devices, shampoo_step(): lax.ppermute(acts[1], 'dp', back)  11.2 us
    ppermute x7, starting transfers between devices, shampoo_step(): down = lax.ppermute(down, 'dp', ahead)  9.43 us
    ppermute x4, waiting for transfers between devices, exchange(): return value + lax.ppermute(value, axis, pairs)  8.78 us
  transfers between devices with their start and end apart: 61, of which 26 were waited for; matrix products, arithmetic and copies ran while one was open for 4% of the time, Pallas kernels for 38%

profile of v2, /device:TPU:0, one launch (start us, length us, event | category | flops | bytes accessed | tf_op | source)
XLA Modules:
  0.0 346.8 jit_solution(1180106227705633490)
XLA Ops:
  1.9 3.0 collective-permute-start.4
  5.1 1.4 fusion.9
  6.5 2.0 collective-permute-start.1
  16.9 2.0 collective-permute-start.5
  19.5 6.0 %collective-permute-done.5.refs_22_ = bf16[512,128]{1,0:T(8,128)(2,1)S(1)} collective-permute-done((bf16[512,128]{1,0:T(8,128)(2,1)S(1)}, bf16[512,128]{1,0:T(8,128)(2,1)S(1)}, u32[]{:S(2)}, u32[]{:S(2)}) %collective-permute-start.5) | collective-permute-done | bytes 131104 | tf_op jit(solution)/shard_map/ppermute | solution.py:398
  25.5 1.4 collective-permute-done.3.refs_21_
  27.4 1.6 collective-permute-start.7
  29.7 1.6 collective-permute-start.9
  34.1 10.4 %collective-permute-done.8.refs_23_ = bf16[512,128]{1,0:T(8,128)(2,1)S(1)} collective-permute-done((bf16[512,128]{1,0:T(8,128)(2,1)}, bf16[512,128]{1,0:T(8,128)(2,1)S(1)}, u32[]{:S(2)}, u32[]{:S(2)}) %collective-permute-start.8) | collective-permute-done | bytes 131104 | tf_op jit(solution)/shard_map/ppermute | solution.py:398
  45.0 1.6 collective-permute-start.10
  47.1 1.5 collective-permute-start.12
  49.1 12.7 %collective-permute-done.12.refs_25_ = bf16[512,128]{1,0:T(8,128)(2,1)S(1)} collective-permute-done((bf16[512,128]{1,0:T(8,128)(2,1)S(1)}, bf16[512,128]{1,0:T(8,128)(2,1)S(1)}, u32[]{:S(2)}, u32[]{:S(2)}) %collective-permute-start.12) | collective-permute-done | bytes 131104 | tf_op jit(solution)/shard_map/ppermute | solution.py:398
  63.2 1.8 collective-permute-start.14
  65.3 1.7 collective-permute-start.16
  67.3 12.7 %collective-permute-done.16.refs_27_ = bf16[512,128]{1,0:T(8,128)(2,1)S(1)} collective-permute-done((bf16[512,128]{1,0:T(8,128)(2,1)S(1)}, bf16[512,128]{1,0:T(8,128)(2,1)S(1)}, u32[]{:S(2)}, u32[]{:S(2)}) %collective-permute-start.16) | collective-permute-done | bytes 131104 | tf_op jit(solution)/shard_map/ppermute | solution.py:398
  80.0 1.5 collective-permute-done.17.refs_28_
  81.5 2.0 collective-permute-start.18
  83.6 1.9 collective-permute-start.20
  85.6 13.0 %collective-permute-done.20.refs_29_ = bf16[512,128]{1,0:T(8,128)(2,1)} collective-permute-done((bf16[512,128]{1,0:T(8,128)(2,1)S(1)}, bf16[512,128]{1,0:T(8,128)(2,1)}, u32[]{:S(2)}, u32[]{:S(2)}) %collective-permute-start.20) | collective-permute-done | bytes 131104 | tf_op jit(solution)/shard_map/ppermute | solution.py:398
  99.6 1.6 collective-permute-start.22
  101.7 1.6 collective-permute-start.24
  103.7 12.6 %collective-permute-done.24.refs_31_ = bf16[512,128]{1,0:T(8,128)(2,1)} collective-permute-done((bf16[512,128]{1,0:T(8,128)(2,1)}, bf16[512,128]{1,0:T(8,128)(2,1)}, u32[]{:S(2)}, u32[]{:S(2)}) %collective-permute-start.24) | collective-permute-done | bytes 131104 | tf_op jit(solution)/shard_map/ppermute | solution.py:398
  117.3 1.8 collective-permute-start.26
  125.7 2.2 collective-permute-done.26.refs_16_
  127.9 1.8 collective-permute-done.27.refs_17_
  130.7 1.7 collective-permute-done.42.refs_47_
  132.5 31.1 %shard_map.113 = (bf16[512,1024]{1,0:T(8,128)(2,1)}, bf16[512,1024]{1,0:T(8,128)(2,1)}, f32[1,1]{1,0:T(1,128)}) custom-call(s32[20]{0:T(128)} %reshape.422.refs_0_, f32[10]{0:T(128)} %reshape.423.refs_1_, s32[16]{0:T(128)} %pad_add_fusion.6.refs_2_, bf16[128,5120]{1,0:T(8,128)(2,1)} %refs_3_.13, bf16[64,5120]{1,0:T(8,128)(2,1)} %copy-done.14, ...), custom_call_target="tpu_custom_call" | custom-call | flops 27917287424 | bytes 12582912 | tf_op jit(solution)/shard_map/pallas_call | solution.py:226
  164.1 1.4 collective-permute-start.43
  165.5 2.4 collective-permute-done.43
  168.5 2.4 collective-permute-start.45
  170.9 14.4 %shard_map.114.refs_48_ = bf16[1024,1024]{1,0:T(8,128)(2,1)} custom-call(s32[20]{0:T(128)} %reshape.422.refs_0_, f32[10]{0:T(128)} %reshape.423.refs_1_, s32[16]{0:T(128)} %pad_add_fusion.6.refs_2_, bf16[128,5120]{1,0:T(8,128)(2,1)} %refs_3_.13, bf16[64,5120]{1,0:T(8,128)(2,1)} %copy-done.14, bf16[64,5120]{1,0:T(8,128)(2,1)} %copy-done.13, ...), custom_call_target="tpu_custom_call" | custom-call | flops 12884901888 | bytes 12582912 | tf_op jit(solution)/shard_map/pallas_call | solution.py:226
  185.3 5.2 %collective-permute-start.46 = (f32[1,1]{1,0:T(1,128)}, f32[1,1]{1,0:T(1,128)}, u32[]{:S(2)}, u32[]{:S(2)}) collective-permute-start(f32[1,1]{1,0:T(1,128)} %add.168), channel_id=1, source_target_pairs={{0,4},{2,6},{4,0},{6,2},{8,12},{10,14},{12,8},{14,10},{1,5},{3,7},... | collective-permute-start | bytes 20 | tf_op jit(solution)/shard_map/ppermute | solution.py:432
  190.5 2.7 collective-permute-done.46
  195.9 20.1 %shard_map.115 = (bf16[512,1024]{1,0:T(8,128)(2,1)}, bf16[512,1024]{1,0:T(8,128)(2,1)}, f32[1,1]{1,0:T(1,128)}) custom-call(s32[20]{0:T(128)} %reshape.422.refs_0_, f32[10]{0:T(128)} %reshape.423.refs_1_, s32[16]{0:T(128)} %pad_add_fusion.6.refs_2_, bf16[128,5120]{1,0:T(8,128)(2,1)} %refs_3_.13, bf16[64,5120]{1,0:T(8,128)(2,1)} %copy-done.14, ...), custom_call_target="tpu_custom_call" | custom-call | flops 17179869184 | bytes 12582912 | tf_op jit(solution)/shard_map/pallas_call | solution.py:226
  216.8 1.5 collective-permute-done.48.refs_49_.refs_11_
  218.4 2.0 collective-permute-start.49
  220.4 14.6 %shard_map.116.refs_48_ = bf16[1024,1024]{1,0:T(8,128)(2,1)} custom-call(s32[20]{0:T(128)} %reshape.422.refs_0_, f32[10]{0:T(128)} %reshape.423.refs_1_, s32[16]{0:T(128)} %pad_add_fusion.6.refs_2_, bf16[128,5120]{1,0:T(8,128)(2,1)} %refs_3_.13, bf16[64,5120]{1,0:T(8,128)(2,1)} %copy-done.14, bf16[64,5120]{1,0:T(8,128)(2,1)} %copy-done.13, ...), custom_call_target="tpu_custom_call" | custom-call | flops 12884901888 | bytes 12582912 | tf_op jit(solution)/shard_map/pallas_call | solution.py:226
  235.0 4.5 %collective-permute-start.51 = (f32[1,1]{1,0:T(1,128)}, f32[1,1]{1,0:T(1,128)}, u32[]{:S(2)}, u32[]{:S(2)}) collective-permute-start(f32[1,1]{1,0:T(1,128)} %add.169), channel_id=1, source_target_pairs={{0,8},{2,10},{4,12},{6,14},{8,0},{10,2},{12,4},{14,6},{1,9},{3,11}... | collective-permute-start | bytes 20 | tf_op jit(solution)/shard_map/ppermute | solution.py:432
  239.5 3.4 collective-permute-done.51
  243.7 2.0 collective-permute-start.53
  245.7 20.3 %shard_map.117 = (bf16[512,1024]{1,0:T(8,128)(2,1)}, bf16[512,1024]{1,0:T(8,128)(2,1)}, f32[1,1]{1,0:T(1,128)}) custom-call(s32[20]{0:T(128)} %reshape.422.refs_0_, f32[10]{0:T(128)} %reshape.423.refs_1_, s32[16]{0:T(128)} %pad_add_fusion.6.refs_2_, bf16[128,5120]{1,0:T(8,128)(2,1)} %refs_3_.13, bf16[64,5120]{1,0:T(8,128)(2,1)} %copy-done.14, ...), custom_call_target="tpu_custom_call" | custom-call | flops 17179869184 | bytes 12582912 | tf_op jit(solution)/shard_map/pallas_call | solution.py:226
  266.2 2.1 collective-permute-start.55
  268.3 23.0 %shard_map.118.refs_48_ = bf16[2,2,1024,1024]{3,2,1,0:T(8,128)(2,1)} custom-call(s32[20]{0:T(128)} %reshape.422.refs_0_, f32[10]{0:T(128)} %reshape.423.refs_1_, s32[16]{0:T(128)} %pad_add_fusion.6.refs_2_, bf16[128,5120]{1,0:T(8,128)(2,1)} %refs_3_.13, bf16[64,5120]{1,0:T(8,128)(2,1)} %copy-done.14, bf16[64,5120]{1,0:T(8,128)(2,1)} %copy-done.13, ...), custom_call_target="tpu_custom_call" | custom-call | flops 23622320128 | bytes 12582912 | tf_op jit(solution)/shard_map/pallas_call | solution.py:226
  291.5 3.5 %collective-permute-start.57 = (bf16[512,1024]{1,0:T(8,128)(2,1)S(1)}, bf16[512,1024]{1,0:T(8,128)(2,1)}, u32[]{:S(2)}, u32[]{:S(2)}) collective-permute-start(bf16[512,1024]{1,0:T(8,128)(2,1)S(1)} %collective-permute-done.55.refs_50_.refs_17_), channel_id=1, source_target_pairs={{4,0},{8,4},{12,8},{14,12},{10,14},{6,10},{2,6},{0,2},{5,1},{9,5},... | collective-permute-start | bytes 3145736 | tf_op jit(solution)/shard_map/ppermute | solution.py:443
  295.0 26.2 %shard_map.119 = bf16[2,2,1024,1024]{3,2,1,0:T(8,128)(2,1)} custom-call(s32[20]{0:T(128)} %reshape.422.refs_0_, f32[10]{0:T(128)} %reshape.423.refs_1_, s32[16]{0:T(128)} %pad_add_fusion.6.refs_2_, bf16[128,5120]{1,0:T(8,128)(2,1)} %refs_3_.13, bf16[64,5120]{1,0:T(8,128)(2,1)} %copy-done.14, ...), custom_call_target="tpu_custom_call", output_to_operand_aliasing={{}: (48, {})} | custom-call | flops 23622320128 | bytes 12582912 | tf_op jit(solution)/shard_map/pallas_call | solution.py:226
  321.3 2.2 collective-permute-start.60
  326.8 14.5 %place.2.refs_4_ = bf16[2048,5120]{1,0:T(8,128)(2,1)} custom-call(s32[40]{0:T(128)} %reshape.424.refs_0_, f32[1,1]{1,0:T(1,128)S(6)} %rsqrt.3.refs_1_, bf16[512,1024]{1,0:T(8,128)(2,1)} %get-tuple-element.100.refs_2_, bf16[512,1024]{1,0:T(8,128)(2,1)} %get-tuple-element.120.refs_3_, bf16[512,1024]{1,0:T(8,128)(2,1)} %get-tuple-element.108.refs_4_, ...), custom_call_target="tpu_custom_call" | custom-call | flops 1887436800 | bytes 37748736 | tf_op jit(solution)/shard_map/place/pallas_call | solution.py:291
  343.4 3.1 place.3
  (213 shorter events, 35.0 us)
Async XLA Ops:
  1.9 14.9 %collective-permute-start.4 = (bf16[512,128]{1,0:T(8,128)(2,1)S(1)}, bf16[512,128]{1,0:T(8,128)(2,1)S(1)}, u32[]{:S(2)}, u32[]{:S(2)}) collective-permute-start(bf16[512,128]{1,0:T(8,128)(2,1)S(1)} %get-tuple-element.128), channel_id=1, source_target_pairs={{4,0},{8,4},{12,8},{14,12},{10,14},{6,10},{2,6},{0,2},{5,1},{9,5},... | collective-permute-start | bytes 393224 | tf_op jit(solution)/shard_map/ppermute | solution.py:398
  5.0 13.9 %collective-permute-start.2 = (bf16[512,128]{1,0:T(8,128)(2,1)S(1)}, bf16[512,128]{1,0:T(8,128)(2,1)S(1)}, u32[]{:S(2)}, u32[]{:S(2)}) collective-permute-start(bf16[512,128]{1,0:T(8,128)(2,1)S(1)} %get-tuple-element.129), channel_id=1, source_target_pairs={{0,4},{4,8},{8,12},{12,14},{14,10},{10,6},{6,2},{2,0},{1,5},{5,9},... | collective-permute-start | bytes 393224 | tf_op jit(solution)/shard_map/ppermute | solution.py:398
  6.5 20.5 %collective-permute-start.1 = (bf16[64,5120]{1,0:T(8,128)(2,1)S(1)}, bf16[64,5120]{1,0:T(8,128)(2,1)S(1)}, u32[]{:S(2)}, u32[]{:S(2)}) collective-permute-start(bf16[64,5120]{1,0:T(8,128)(2,1)S(1)} %get-tuple-element.126), channel_id=1, source_target_pairs={{4,0},{8,4},{12,8},{14,12},{10,14},{6,10},{2,6},{0,2},{5,1},{9,5},... | collective-permute-start | bytes 1966088 | tf_op jit(solution)/shard_map/ppermute | solution.py:395
  8.4 18.6 %collective-permute-start = (bf16[64,5120]{1,0:T(8,128)(2,1)S(1)}, bf16[64,5120]{1,0:T(8,128)(2,1)S(1)}, u32[]{:S(2)}, u32[]{:S(2)}) collective-permute-start(bf16[64,5120]{1,0:T(8,128)(2,1)S(1)} %get-tuple-element.127), channel_id=1, source_target_pairs={{0,4},{4,8},{8,12},{12,14},{14,10},{10,6},{6,2},{2,0},{1,5},{5,9},... | collective-permute-start | bytes 1966088 | tf_op jit(solution)/shard_map/ppermute | solution.py:394
  16.9 8.7 %collective-permute-start.5 = (bf16[512,128]{1,0:T(8,128)(2,1)S(1)}, bf16[512,128]{1,0:T(8,128)(2,1)S(1)}, u32[]{:S(2)}, u32[]{:S(2)}) collective-permute-start(bf16[512,128]{1,0:T(8,128)(2,1)S(1)} %collective-permute-done.4.refs_20_), channel_id=1, source_target_pairs={{4,0},{8,4},{12,8},{14,12},{10,14},{6,10},{2,6},{0,2},{5,1},{9,5},... | collective-permute-start | bytes 393224 | tf_op jit(solution)/shard_map/ppermute | solution.py:398
  18.8 8.1 %collective-permute-start.3 = (bf16[512,128]{1,0:T(8,128)(2,1)S(1)}, bf16[512,128]{1,0:T(8,128)(2,1)}, u32[]{:S(2)}, u32[]{:S(2)}) collective-permute-start(bf16[512,128]{1,0:T(8,128)(2,1)S(1)} %collective-permute-done.2.refs_19_), channel_id=1, source_target_pairs={{0,4},{4,8},{8,12},{12,14},{14,10},{10,6},{6,2},{2,0},{1,5},{5,9},... | collective-permute-start | bytes 393224 | tf_op jit(solution)/shard_map/ppermute | solution.py:398
  27.0 18.0 %collective-permute-start.6 = (bf16[64,5120]{1,0:T(8,128)(2,1)S(1)}, bf16[64,5120]{1,0:T(8,128)(2,1)S(1)}, u32[]{:S(2)}, u32[]{:S(2)}) collective-permute-start(bf16[64,5120]{1,0:T(8,128)(2,1)S(1)} %collective-permute-done.refs_4_), channel_id=1, source_target_pairs={{0,4},{4,8},{8,12},{12,14},{14,10},{10,6},{6,2},{2,0},{1,5},{5,9},... | collective-permute-start | bytes 1966088 | tf_op jit(solution)/shard_map/ppermute | solution.py:394
  27.4 17.6 %collective-permute-start.7 = (bf16[64,5120]{1,0:T(8,128)(2,1)S(1)}, bf16[64,5120]{1,0:T(8,128)(2,1)}, u32[]{:S(2)}, u32[]{:S(2)}) collective-permute-start(bf16[64,5120]{1,0:T(8,128)(2,1)S(1)} %collective-permute-done.1.refs_5_), channel_id=1, source_target_pairs={{4,0},{8,4},{12,8},{14,12},{10,14},{6,10},{2,6},{0,2},{5,1},{9,5},... | collective-permute-start | bytes 1966088 | tf_op jit(solution)/shard_map/ppermute | solution.py:395
  29.2 15.3 %collective-permute-start.8 = (bf16[512,128]{1,0:T(8,128)(2,1)}, bf16[512,128]{1,0:T(8,128)(2,1)S(1)}, u32[]{:S(2)}, u32[]{:S(2)}) collective-permute-start(bf16[512,128]{1,0:T(8,128)(2,1)} %collective-permute-done.3.refs_21_), channel_id=1, source_target_pairs={{0,4},{4,8},{8,12},{12,14},{14,10},{10,6},{6,2},{2,0},{1,5},{5,9},... | collective-permute-start | bytes 393224 | tf_op jit(solution)/shard_map/ppermute | solution.py:398
  29.7 15.3 %collective-permute-start.9 = (bf16[512,128]{1,0:T(8,128)(2,1)S(1)}, bf16[512,128]{1,0:T(8,128)(2,1)}, u32[]{:S(2)}, u32[]{:S(2)}) collective-permute-start(bf16[512,128]{1,0:T(8,128)(2,1)S(1)} %collective-permute-done.5.refs_22_), channel_id=1, source_target_pairs={{4,0},{8,4},{12,8},{14,12},{10,14},{6,10},{2,6},{0,2},{5,1},{9,5},... | collective-permute-start | bytes 393224 | tf_op jit(solution)/shard_map/ppermute | solution.py:398
  45.0 18.1 %collective-permute-start.10 = (bf16[64,5120]{1,0:T(8,128)(2,1)S(1)}, bf16[64,5120]{1,0:T(8,128)(2,1)S(1)}, u32[]{:S(2)}, u32[]{:S(2)}) collective-permute-start(bf16[64,5120]{1,0:T(8,128)(2,1)S(1)} %collective-permute-done.6.refs_6_), channel_id=1, source_target_pairs={{0,4},{4,8},{8,12},{12,14},{14,10},{10,6},{6,2},{2,0},{1,5},{5,9},... | collective-permute-start | bytes 1966088 | tf_op jit(solution)/shard_map/ppermute | solution.py:394
  46.6 16.6 %collective-permute-start.11 = (bf16[64,5120]{1,0:T(8,128)(2,1)}, bf16[64,5120]{1,0:T(8,128)(2,1)S(1)}, u32[]{:S(2)}, u32[]{:S(2)}) collective-permute-start(bf16[64,5120]{1,0:T(8,128)(2,1)} %collective-permute-done.7.refs_7_), channel_id=1, source_target_pairs={{4,0},{8,4},{12,8},{14,12},{10,14},{6,10},{2,6},{0,2},{5,1},{9,5},... | collective-permute-start | bytes 1966088 | tf_op jit(solution)/shard_map/ppermute | solution.py:395
  47.1 14.7 %collective-permute-start.12 = (bf16[512,128]{1,0:T(8,128)(2,1)S(1)}, bf16[512,128]{1,0:T(8,128)(2,1)S(1)}, u32[]{:S(2)}, u32[]{:S(2)}) collective-permute-start(bf16[512,128]{1,0:T(8,128)(2,1)S(1)} %collective-permute-done.8.refs_23_), channel_id=1, source_target_pairs={{0,4},{4,8},{8,12},{12,14},{14,10},{10,6},{6,2},{2,0},{1,5},{5,9},... | collective-permute-start | bytes 393224 | tf_op jit(solution)/shard_map/ppermute | solution.py:398
  48.6 14.5 %collective-permute-start.13 = (bf16[512,128]{1,0:T(8,128)(2,1)}, bf16[512,128]{1,0:T(8,128)(2,1)S(1)}, u32[]{:S(2)}, u32[]{:S(2)}) collective-permute-start(bf16[512,128]{1,0:T(8,128)(2,1)} %collective-permute-done.9.refs_24_), channel_id=1, source_target_pairs={{4,0},{8,4},{12,8},{14,12},{10,14},{6,10},{2,6},{0,2},{5,1},{9,5},... | collective-permute-start | bytes 393224 | tf_op jit(solution)/shard_map/ppermute | solution.py:398
  63.2 18.3 %collective-permute-start.14 = (bf16[64,5120]{1,0:T(8,128)(2,1)S(1)}, bf16[64,5120]{1,0:T(8,128)(2,1)S(1)}, u32[]{:S(2)}, u32[]{:S(2)}) collective-permute-start(bf16[64,5120]{1,0:T(8,128)(2,1)S(1)} %collective-permute-done.10.refs_8_), channel_id=1, source_target_pairs={{0,4},{4,8},{8,12},{12,14},{14,10},{10,6},{6,2},{2,0},{1,5},{5,9},... | collective-permute-start | bytes 1966088 | tf_op jit(solution)/shard_map/ppermute | solution.py:394
  65.0 16.5 %collective-permute-start.15 = (bf16[64,5120]{1,0:T(8,128)(2,1)S(1)}, bf16[64,5120]{1,0:T(8,128)(2,1)S(1)}, u32[]{:S(2)}, u32[]{:S(2)}) collective-permute-start(bf16[64,5120]{1,0:T(8,128)(2,1)S(1)} %collective-permute-done.11.refs_9_), channel_id=1, source_target_pairs={{4,0},{8,4},{12,8},{14,12},{10,14},{6,10},{2,6},{0,2},{5,1},{9,5},... | collective-permute-start | bytes 1966088 | tf_op jit(solution)/shard_map/ppermute | solution.py:395
  65.3 14.7 %collective-permute-start.16 = (bf16[512,128]{1,0:T(8,128)(2,1)S(1)}, bf16[512,128]{1,0:T(8,128)(2,1)S(1)}, u32[]{:S(2)}, u32[]{:S(2)}) collective-permute-start(bf16[512,128]{1,0:T(8,128)(2,1)S(1)} %collective-permute-done.12.refs_25_), channel_id=1, source_target_pairs={{0,4},{4,8},{8,12},{12,14},{14,10},{10,6},{6,2},{2,0},{1,5},{5,9},... | collective-permute-start | bytes 393224 | tf_op jit(solution)/shard_map/ppermute | solution.py:398
  67.0 14.5 %collective-permute-start.17 = (bf16[512,128]{1,0:T(8,128)(2,1)S(1)}, bf16[512,128]{1,0:T(8,128)(2,1)}, u32[]{:S(2)}, u32[]{:S(2)}) collective-permute-start(bf16[512,128]{1,0:T(8,128)(2,1)S(1)} %collective-permute-done.13.refs_26_), channel_id=1, source_target_pairs={{4,0},{8,4},{12,8},{14,12},{10,14},{6,10},{2,6},{0,2},{5,1},{9,5},... | collective-permute-start | bytes 393224 | tf_op jit(solution)/shard_map/ppermute | solution.py:398
  81.5 18.1 %collective-permute-start.18 = (bf16[64,5120]{1,0:T(8,128)(2,1)S(1)}, bf16[64,5120]{1,0:T(8,128)(2,1)S(1)}, u32[]{:S(2)}, u32[]{:S(2)}) collective-permute-start(bf16[64,5120]{1,0:T(8,128)(2,1)S(1)} %collective-permute-done.14.refs_10_), channel_id=1, source_target_pairs={{0,4},{4,8},{8,12},{12,14},{14,10},{10,6},{6,2},{2,0},{1,5},{5,9},... | collective-permute-start | bytes 1966088 | tf_op jit(solution)/shard_map/ppermute | solution.py:394
  83.5 16.1 %collective-permute-start.19 = (bf16[64,5120]{1,0:T(8,128)(2,1)S(1)}, bf16[64,5120]{1,0:T(8,128)(2,1)S(1)}, u32[]{:S(2)}, u32[]{:S(2)}) collective-permute-start(bf16[64,5120]{1,0:T(8,128)(2,1)S(1)} %collective-permute-done.15.refs_11_), channel_id=1, source_target_pairs={{4,0},{8,4},{12,8},{14,12},{10,14},{6,10},{2,6},{0,2},{5,1},{9,5},... | collective-permute-start | bytes 1966088 | tf_op jit(solution)/shard_map/ppermute | solution.py:395
  83.6 15.0 %collective-permute-start.20 = (bf16[512,128]{1,0:T(8,128)(2,1)S(1)}, bf16[512,128]{1,0:T(8,128)(2,1)}, u32[]{:S(2)}, u32[]{:S(2)}) collective-permute-start(bf16[512,128]{1,0:T(8,128)(2,1)S(1)} %collective-permute-done.16.refs_27_), channel_id=1, source_target_pairs={{0,4},{4,8},{8,12},{12,14},{14,10},{10,6},{6,2},{2,0},{1,5},{5,9},... | collective-permute-start | bytes 393224 | tf_op jit(solution)/shard_map/ppermute | solution.py:398
  85.5 14.0 %collective-permute-start.21 = (bf16[512,128]{1,0:T(8,128)(2,1)}, bf16[512,128]{1,0:T(8,128)(2,1)}, u32[]{:S(2)}, u32[]{:S(2)}) collective-permute-start(bf16[512,128]{1,0:T(8,128)(2,1)} %collective-permute-done.17.refs_28_), channel_id=1, source_target_pairs={{4,0},{8,4},{12,8},{14,12},{10,14},{6,10},{2,6},{0,2},{5,1},{9,5},... | collective-permute-start | bytes 393224 | tf_op jit(solution)/shard_map/ppermute | solution.py:398
  99.6 17.7 %collective-permute-start.22 = (bf16[64,5120]{1,0:T(8,128)(2,1)S(1)}, bf16[64,5120]{1,0:T(8,128)(2,1)S(1)}, u32[]{:S(2)}, u32[]{:S(2)}) collective-permute-start(bf16[64,5120]{1,0:T(8,128)(2,1)S(1)} %collective-permute-done.18.refs_12_), channel_id=1, source_target_pairs={{0,4},{4,8},{8,12},{12,14},{14,10},{10,6},{6,2},{2,0},{1,5},{5,9},... | collective-permute-start | bytes 1966088 | tf_op jit(solution)/shard_map/ppermute | solution.py:394
  101.2 16.1 %collective-permute-start.23 = (bf16[64,5120]{1,0:T(8,128)(2,1)S(1)}, bf16[64,5120]{1,0:T(8,128)(2,1)S(1)}, u32[]{:S(2)}, u32[]{:S(2)}) collective-permute-start(bf16[64,5120]{1,0:T(8,128)(2,1)S(1)} %collective-permute-done.19.refs_13_), channel_id=1, source_target_pairs={{4,0},{8,4},{12,8},{14,12},{10,14},{6,10},{2,6},{0,2},{5,1},{9,5},... | collective-permute-start | bytes 1966088 | tf_op jit(solution)/shard_map/ppermute | solution.py:395
  101.7 14.7 %collective-permute-start.24 = (bf16[512,128]{1,0:T(8,128)(2,1)}, bf16[512,128]{1,0:T(8,128)(2,1)}, u32[]{:S(2)}, u32[]{:S(2)}) collective-permute-start(bf16[512,128]{1,0:T(8,128)(2,1)} %collective-permute-done.20.refs_29_), channel_id=1, source_target_pairs={{0,4},{4,8},{8,12},{12,14},{14,10},{10,6},{6,2},{2,0},{1,5},{5,9},... | collective-permute-start | bytes 393224 | tf_op jit(solution)/shard_map/ppermute | solution.py:398
  103.2 14.0 %collective-permute-start.25 = (bf16[512,128]{1,0:T(8,128)(2,1)}, bf16[512,128]{1,0:T(8,128)(2,1)}, u32[]{:S(2)}, u32[]{:S(2)}) collective-permute-start(bf16[512,128]{1,0:T(8,128)(2,1)} %collective-permute-done.21.refs_30_), channel_id=1, source_target_pairs={{4,0},{8,4},{12,8},{14,12},{10,14},{6,10},{2,6},{0,2},{5,1},{9,5},... | collective-permute-start | bytes 393224 | tf_op jit(solution)/shard_map/ppermute | solution.py:398
  117.3 10.6 %collective-permute-start.26 = (bf16[64,5120]{1,0:T(8,128)(2,1)S(1)}, bf16[64,5120]{1,0:T(8,128)(2,1)S(1)}, u32[]{:S(2)}, u32[]{:S(2)}) collective-permute-start(bf16[64,5120]{1,0:T(8,128)(2,1)S(1)} %collective-permute-done.22.refs_14_), channel_id=1, source_target_pairs={{0,4},{4,8},{8,12},{12,14},{14,10},{10,6},{6,2},{2,0},{1,5},{5,9},... | collective-permute-start | bytes 1966088 | tf_op jit(solution)/shard_map/ppermute | solution.py:394
  119.1 10.6 %collective-permute-start.27 = (bf16[64,5120]{1,0:T(8,128)(2,1)S(1)}, bf16[64,5120]{1,0:T(8,128)(2,1)S(1)}, u32[]{:S(2)}, u32[]{:S(2)}) collective-permute-start(bf16[64,5120]{1,0:T(8,128)(2,1)S(1)} %collective-permute-done.23.refs_15_), channel_id=1, source_target_pairs={{4,0},{8,4},{12,8},{14,12},{10,14},{6,10},{2,6},{0,2},{5,1},{9,5},... | collective-permute-start | bytes 1966088 | tf_op jit(solution)/shard_map/ppermute | solution.py:395
  124.4 6.3 %collective-permute-start.38 = (bf16[512,128]{1,0:T(8,128)(2,1)}, bf16[512,128]{1,0:T(8,128)(2,1)}, u32[]{:S(2)}, u32[]{:S(2)}) collective-permute-start(bf16[512,128]{1,0:T(8,128)(2,1)} %collective-permute-done.17.refs_28_), channel_id=1, source_target_pairs={{0,1},{1,0},{2,3},{3,2},{4,5},{5,4},{6,7},{7,6},{8,9},{9,8},{10,11... | collective-permute-start | bytes 393224 | tf_op jit(solution)/shard_map/ppermute | solution.py:401
  124.7 6.0 %collective-permute-start.39 = (bf16[512,128]{1,0:T(8,128)(2,1)}, bf16[512,128]{1,0:T(8,128)(2,1)}, u32[]{:S(2)}, u32[]{:S(2)}) collective-permute-start(bf16[512,128]{1,0:T(8,128)(2,1)} %collective-permute-done.20.refs_29_), channel_id=1, source_target_pairs={{0,1},{1,0},{2,3},{3,2},{4,5},{5,4},{6,7},{7,6},{8,9},{9,8},{10,11... | collective-permute-start | bytes 393224 | tf_op jit(solution)/shard_map/ppermute | solution.py:401
  125.6 5.1 %collective-permute-start.40 = (bf16[512,128]{1,0:T(8,128)(2,1)}, bf16[512,128]{1,0:T(8,128)(2,1)}, u32[]{:S(2)}, u32[]{:S(2)}) collective-permute-start(bf16[512,128]{1,0:T(8,128)(2,1)} %collective-permute-done.21.refs_30_), channel_id=1, source_target_pairs={{0,1},{1,0},{2,3},{3,2},{4,5},{5,4},{6,7},{7,6},{8,9},{9,8},{10,11... | collective-permute-start | bytes 393224 | tf_op jit(solution)/shard_map/ppermute | solution.py:401
  164.1 3.7 %collective-permute-start.43 = (f32[1,1]{1,0:T(1,128)}, f32[1,1]{1,0:T(1,128)}, u32[]{:S(2)}, u32[]{:S(2)}) collective-permute-start(f32[1,1]{1,0:T(1,128)} %select_n.161), channel_id=1, source_target_pairs={{0,2},{2,0},{4,6},{6,4},{8,10},{10,8},{12,14},{14,12},{1,3},{3,1},... | collective-permute-start | bytes 20 | tf_op jit(solution)/shard_map/ppermute | solution.py:432
  168.4 25.3 %collective-permute-start.44 = (bf16[512,1024]{1,0:T(8,128)(2,1)}, bf16[512,1024]{1,0:T(8,128)(2,1)S(1)}, u32[]{:S(2)}, u32[]{:S(2)}) collective-permute-start(bf16[512,1024]{1,0:T(8,128)(2,1)} %get-tuple-element.93.refs_6_), channel_id=1, source_target_pairs={{0,4},{4,8},{8,12},{12,14},{14,10},{10,6},{6,2},{2,0},{1,5},{5,9},... | collective-permute-start | bytes 3145736 | tf_op jit(solution)/shard_map/ppermute | solution.py:442
  168.5 25.3 %collective-permute-start.45 = (bf16[512,1024]{1,0:T(8,128)(2,1)}, bf16[512,1024]{1,0:T(8,128)(2,1)S(1)}, u32[]{:S(2)}, u32[]{:S(2)}) collective-permute-start(bf16[512,1024]{1,0:T(8,128)(2,1)} %get-tuple-element.94.refs_7_), channel_id=1, source_target_pairs={{4,0},{8,4},{12,8},{14,12},{10,14},{6,10},{2,6},{0,2},{5,1},{9,5},... | collective-permute-start | bytes 3145736 | tf_op jit(solution)/shard_map/ppermute | solution.py:443
  185.3 7.9 %collective-permute-start.46 = (f32[1,1]{1,0:T(1,128)}, f32[1,1]{1,0:T(1,128)}, u32[]{:S(2)}, u32[]{:S(2)}) collective-permute-start(f32[1,1]{1,0:T(1,128)} %add.168), channel_id=1, source_target_pairs={{0,4},{2,6},{4,0},{6,2},{8,12},{10,14},{12,8},{14,10},{1,5},{3,7},... | collective-permute-start | bytes 20 | tf_op jit(solution)/shard_map/ppermute | solution.py:432
  193.8 23.0 %collective-permute-start.47 = (bf16[512,1024]{1,0:T(8,128)(2,1)S(1)}, bf16[512,1024]{1,0:T(8,128)(2,1)S(1)}, u32[]{:S(2)}, u32[]{:S(2)}) collective-permute-start(bf16[512,1024]{1,0:T(8,128)(2,1)S(1)} %collective-permute-done.44.refs_49_.refs_8_), channel_id=1, source_target_pairs={{0,4},{4,8},{8,12},{12,14},{14,10},{10,6},{6,2},{2,0},{1,5},{5,9},... | collective-permute-start | bytes 3145736 | tf_op jit(solution)/shard_map/ppermute | solution.py:442
  195.1 23.3 %collective-permute-start.48 = (bf16[512,1024]{1,0:T(8,128)(2,1)S(1)}, bf16[512,1024]{1,0:T(8,128)(2,1)}, u32[]{:S(2)}, u32[]{:S(2)}) collective-permute-start(bf16[512,1024]{1,0:T(8,128)(2,1)S(1)} %collective-permute-done.45.refs_50_.refs_9_), channel_id=1, source_target_pairs={{4,0},{8,4},{12,8},{14,12},{10,14},{6,10},{2,6},{0,2},{5,1},{9,5},... | collective-permute-start | bytes 3145736 | tf_op jit(solution)/shard_map/ppermute | solution.py:443
  218.4 25.2 %collective-permute-start.49 = (bf16[512,1024]{1,0:T(8,128)(2,1)S(1)}, bf16[512,1024]{1,0:T(8,128)(2,1)S(1)}, u32[]{:S(2)}, u32[]{:S(2)}) collective-permute-start(bf16[512,1024]{1,0:T(8,128)(2,1)S(1)} %collective-permute-done.47.refs_48_.refs_10_), channel_id=1, source_target_pairs={{0,4},{4,8},{8,12},{12,14},{14,10},{10,6},{6,2},{2,0},{1,5},{5,9},... | collective-permute-start | bytes 3145736 | tf_op jit(solution)/shard_map/ppermute | solution.py:442
  220.4 23.2 %collective-permute-start.50 = (bf16[512,1024]{1,0:T(8,128)(2,1)}, bf16[512,1024]{1,0:T(8,128)(2,1)S(1)}, u32[]{:S(2)}, u32[]{:S(2)}) collective-permute-start(bf16[512,1024]{1,0:T(8,128)(2,1)} %collective-permute-done.48.refs_49_.refs_11_), channel_id=1, source_target_pairs={{4,0},{8,4},{12,8},{14,12},{10,14},{6,10},{2,6},{0,2},{5,1},{9,5},... | collective-permute-start | bytes 3145736 | tf_op jit(solution)/shard_map/ppermute | solution.py:443
  235.0 7.9 %collective-permute-start.51 = (f32[1,1]{1,0:T(1,128)}, f32[1,1]{1,0:T(1,128)}, u32[]{:S(2)}, u32[]{:S(2)}) collective-permute-start(f32[1,1]{1,0:T(1,128)} %add.169), channel_id=1, source_target_pairs={{0,8},{2,10},{4,12},{6,14},{8,0},{10,2},{12,4},{14,6},{1,9},{3,11}... | collective-permute-start | bytes 20 | tf_op jit(solution)/shard_map/ppermute | solution.py:432
  243.6 22.4 %collective-permute-start.52 = (bf16[512,1024]{1,0:T(8,128)(2,1)S(1)}, bf16[512,1024]{1,0:T(8,128)(2,1)S(1)}, u32[]{:S(2)}, u32[]{:S(2)}) collective-permute-start(bf16[512,1024]{1,0:T(8,128)(2,1)S(1)} %collective-permute-done.49.refs_49_.refs_12_), channel_id=1, source_target_pairs={{0,4},{4,8},{8,12},{12,14},{14,10},{10,6},{6,2},{2,0},{1,5},{5,9},... | collective-permute-start | bytes 3145736 | tf_op jit(solution)/shard_map/ppermute | solution.py:442
  243.7 22.3 %collective-permute-start.53 = (bf16[512,1024]{1,0:T(8,128)(2,1)S(1)}, bf16[512,1024]{1,0:T(8,128)(2,1)}, u32[]{:S(2)}, u32[]{:S(2)}) collective-permute-start(bf16[512,1024]{1,0:T(8,128)(2,1)S(1)} %collective-permute-done.50.refs_50_.refs_13_), channel_id=1, source_target_pairs={{4,0},{8,4},{12,8},{14,12},{10,14},{6,10},{2,6},{0,2},{5,1},{9,5},... | collective-permute-start | bytes 3145736 | tf_op jit(solution)/shard_map/ppermute | solution.py:443
  266.0 25.3 %collective-permute-start.54 = (bf16[512,1024]{1,0:T(8,128)(2,1)S(1)}, bf16[512,1024]{1,0:T(8,128)(2,1)S(1)}, u32[]{:S(2)}, u32[]{:S(2)}) collective-permute-start(bf16[512,1024]{1,0:T(8,128)(2,1)S(1)} %collective-permute-done.52.refs_48_.refs_14_), channel_id=1, source_target_pairs={{0,4},{4,8},{8,12},{12,14},{14,10},{10,6},{6,2},{2,0},{1,5},{5,9},... | collective-permute-start | bytes 3145736 | tf_op jit(solution)/shard_map/ppermute | solution.py:442
  266.2 25.2 %collective-permute-start.55 = (bf16[512,1024]{1,0:T(8,128)(2,1)}, bf16[512,1024]{1,0:T(8,128)(2,1)S(1)}, u32[]{:S(2)}, u32[]{:S(2)}) collective-permute-start(bf16[512,1024]{1,0:T(8,128)(2,1)} %collective-permute-done.53.refs_49_.refs_15_), channel_id=1, source_target_pairs={{4,0},{8,4},{12,8},{14,12},{10,14},{6,10},{2,6},{0,2},{5,1},{9,5},... | collective-permute-start | bytes 3145736 | tf_op jit(solution)/shard_map/ppermute | solution.py:443
  291.3 29.8 %collective-permute-start.56 = (bf16[512,1024]{1,0:T(8,128)(2,1)S(1)}, bf16[512,1024]{1,0:T(8,128)(2,1)S(1)}, u32[]{:S(2)}, u32[]{:S(2)}) collective-permute-start(bf16[512,1024]{1,0:T(8,128)(2,1)S(1)} %collective-permute-done.54.refs_49_.refs_16_), channel_id=1, source_target_pairs={{0,4},{4,8},{8,12},{12,14},{14,10},{10,6},{6,2},{2,0},{1,5},{5,9},... | collective-permute-start | bytes 3145736 | tf_op jit(solution)/shard_map/ppermute | solution.py:442
  291.5 29.7 %collective-permute-start.57 = (bf16[512,1024]{1,0:T(8,128)(2,1)S(1)}, bf16[512,1024]{1,0:T(8,128)(2,1)}, u32[]{:S(2)}, u32[]{:S(2)}) collective-permute-start(bf16[512,1024]{1,0:T(8,128)(2,1)S(1)} %collective-permute-done.55.refs_50_.refs_17_), channel_id=1, source_target_pairs={{4,0},{8,4},{12,8},{14,12},{10,14},{6,10},{2,6},{0,2},{5,1},{9,5},... | collective-permute-start | bytes 3145736 | tf_op jit(solution)/shard_map/ppermute | solution.py:443
  321.2 20.1 %collective-permute-start.59 = (bf16[512,1024]{1,0:T(8,128)(2,1)S(1)}, bf16[512,1024]{1,0:T(8,128)(2,1)S(1)}, u32[]{:S(2)}, u32[]{:S(2)}) collective-permute-start(bf16[512,1024]{1,0:T(8,128)(2,1)S(1)} %collective-permute-done.56.refs_18_), channel_id=1, source_target_pairs={{0,4},{4,8},{8,12},{12,14},{14,10},{10,6},{6,2},{2,0},{1,5},{5,9},... | collective-permute-start | bytes 3145736 | tf_op jit(solution)/shard_map/ppermute | solution.py:442
  321.3 22.1 %collective-permute-start.60 = (bf16[512,1024]{1,0:T(8,128)(2,1)}, bf16[512,1024]{1,0:T(8,128)(2,1)}, u32[]{:S(2)}, u32[]{:S(2)}) collective-permute-start(bf16[512,1024]{1,0:T(8,128)(2,1)} %collective-permute-done.57.refs_19_), channel_id=1, source_target_pairs={{4,0},{8,4},{12,8},{14,12},{10,14},{6,10},{2,6},{0,2},{5,1},{9,5},... | collective-permute-start | bytes 3145736 | tf_op jit(solution)/shard_map/ppermute | solution.py:443
  (56 other events, 1421.7 us)
